TPU v7x, 512 devices: a whole 4x8x8 slice. The times are simulated.
512 devices in a mesh: tm: 8 (over x, core), lat: 16 (over y, z_hi), lon: 4 (over z_lo).
Axes of the slice: x: 4, y: 8, z: 8 (z_hi: 2, z_lo: 4; z = z_hi * 4 + z_lo), core: 2. Of those that a mesh axis runs over, the one named last changes fastest.
Arguments:
- control: float32 [16, 8, 256, 512], P(None, None, 'lat', 'lon'), may hold values from -6 to 6
- ens_pert: bfloat16 [8, 16, 8, 256, 512], P('tm', None, None, 'lat', 'lon'), may hold values from -6 to 6
- lat_filter: bfloat16 [256, 256], replicated, may hold values from 0 to 2.5, as said below
- lon_filter: bfloat16 [512, 512], replicated, may hold values from 0 to 2.5, as said below
- interp_lat: float32 [512, 18], P('lat'), may hold values from -1.5 to 1.5
- interp_lon: float32 [1024, 130], P('lon'), may hold values from -0.5 to 0.5
- obs_cell: int32 [8, 8, 16, 4, 64], P('tm', None, 'lat', 'lon'), may hold values from 0 to 65535
- obs_count: int32 [8, 8, 16, 4], P('tm', None, 'lat', 'lon'), may hold values from 1 to 64, as said below
- obs_value: float32 [8, 8, 16, 4, 64], P('tm', None, 'lat', 'lon'), may hold values from -18 to 18
- obs_weight: float32 [8, 8, 16, 4, 64], P('tm', None, 'lat', 'lon'), may hold values from 0.1 to 0.4
Outputs:
- gradient: float32 [16, 8, 256, 512], P(None, None, 'lat', 'lon')
Inputs may be any that keep to these rules, and one draw needn't show every extreme that they name: `lat_filter`: within the latitude spreading matrix all entries are non-negative. `lon_filter`: entries are non-negative. `obs_count`: each count is at least 1 and at most 64; in every draw some count equals 64.
All inputs are finite; a program needn't handle non-finite values.
Results may differ from a plain program's by a relative error of at most 0.0003.
Values sent between devices are 32-bit elements; how exact they have to be, the bound alone decides.
A program may use at most 64 MiB of HBM per device.

v0:
```python
import jax
import jax.numpy as jnp
from jax import lax
from jax.sharding import PartitionSpec as P

HIGHEST = lax.Precision.HIGHEST
DIRECTIONS = ((-1, -1), (-1, 0), (-1, 1), (0, -1), (0, 1), (1, -1), (1, 0), (1, 1))


def sent_to_all(array, axis):
    size = lax.axis_size(axis)
    return lax.all_to_all(
        jnp.broadcast_to(array[None], (size, *array.shape)), axis, 0, 0, tiled=True
    )


def in_order(blocks, dim):
    blocks = jnp.moveaxis(blocks, 0, dim)
    dims = blocks.shape
    return blocks.reshape(*dims[:dim], dims[dim] * dims[dim + 1], *dims[dim + 2 :])


def gathered_copies(array, axis, dim):
    blocks = sent_to_all(array, axis)
    return in_order(blocks, dim)


def extended(array, sides, width):
    for axis, dim in sides:
        size, length = (lax.axis_size(axis), array.shape[dim])
        up = [(i, (i + 1) % size) for i in range(size)]
        down = [(j, i) for i, j in up]
        last = lax.slice_in_dim(array, length - width, length, axis=dim)
        first = lax.slice_in_dim(array, 0, width, axis=dim)
        before = lax.ppermute(last, axis, up)
        after = lax.ppermute(first, axis, down)
        array = jnp.concatenate([before, array, after], axis=dim)
    return array


def split_up(array, dim, size):
    before, after = (array.shape[:dim], array.shape[dim + 1 :])
    return jnp.moveaxis(array.reshape(*before, size, -1, *after), dim, 0)


def summed_on_arrival(array, axis, dim):
    size = lax.axis_size(axis)
    blocks = lax.all_to_all(split_up(array, dim, size), axis, 0, 0, tiled=True)
    return jnp.sum(blocks, axis=0)


def spread_field(source, lat_matrix, lon_matrix):
    members, levels, lat_rows, lon_cols = source.shape
    fields = members * levels
    stacked = source.reshape(fields, lat_rows, lon_cols)
    across = jnp.einsum(
        "ab,mbk->mak",
        lat_matrix,
        lax.all_to_all(stacked, "lat", split_axis=0, concat_axis=1, tiled=True),
        precision=HIGHEST,
    )
    halfway = lax.all_to_all(across, "lat", split_axis=1, concat_axis=0, tiled=True)
    column = lax.axis_index("lon") * lon_cols
    portion = lax.all_gather(halfway, "lon", axis=2, tiled=True)
    section = lax.dynamic_slice(lon_matrix, (column, 0), (lon_cols, portion.shape[2]))
    result = jnp.einsum("mak,ck->mac", portion, section, precision=HIGHEST)
    return result.reshape(members, levels, lat_rows, lon_cols)


def rim_region(offset, length):
    if offset < 0:
        return slice(0, 1)
    if offset > 0:
        return slice(length + 1, length + 2)
    return slice(1, length + 1)


def own_cells(offset, length):
    if offset < 0:
        return slice(0, 1)
    if offset > 0:
        return slice(length - 1, length)
    return slice(0, length)


def per_device(
    control,
    ens_pert,
    lat_filter,
    lon_filter,
    interp_lat,
    interp_lon,
    obs_cell,
    obs_count,
    obs_value,
    obs_weight,
):
    lat_matrix = lat_filter.astype(jnp.float32)
    lon_matrix = lon_filter.astype(jnp.float32)
    members = control.shape[0]
    slot_pert = ens_pert[0]
    share = members // lax.axis_size("tm")
    first = lax.axis_index("tm") * share
    mine = lax.dynamic_slice_in_dim(control, first, share, 0)
    spread_mine = spread_field(mine, lat_matrix, lon_matrix)
    weights_here = slot_pert.astype(jnp.float32)
    increment = jnp.sum(gathered_copies(spread_mine, "tm", 0) * weights_here, axis=0)
    levels, lat_rows, lon_cols = increment.shape
    padded = extended(increment, (("lat", 1), ("lon", 2)), 1)
    lat_band = lax.axis_index("lat")
    edge_rows = jnp.arange(lat_rows + 2)
    dropped = (edge_rows == 0) & (lat_band == 0) | (edge_rows == lat_rows + 1) & (
        lat_band == lax.axis_size("lat") - 1
    )
    keeping = jnp.logical_not(dropped).astype(jnp.float32)[None, :, None]
    padded = padded * keeping
    rowwise = jnp.einsum("ip,lpq->liq", interp_lat, padded, precision=HIGHEST)
    finer = jnp.einsum("liq,jq->lij", rowwise, interp_lon, precision=HIGHEST)
    fine_rows = finer.shape[1]
    fine_cols = finer.shape[2]
    flat_field = finer.reshape(-1)
    slots_range = jnp.arange(obs_cell.shape[-1])
    usable = (slots_range < obs_count[..., None]).astype(jnp.float32)
    package = jnp.stack([obs_cell.astype(jnp.float32), obs_value, obs_weight * usable], axis=0)
    arrived = lax.all_to_all(package, "tm", split_axis=2, concat_axis=1, tiled=True)
    places = arrived[0].reshape(-1).astype(jnp.int32)
    targets = arrived[1].reshape(-1)
    weights = arrived[2].reshape(-1)
    seen = flat_field[places]
    departure = weights * (seen - targets)
    fine_grad = jnp.zeros_like(flat_field).at[places].add(departure)
    fine_grad = fine_grad.reshape(levels, fine_rows, fine_cols)
    pulled = jnp.einsum("jq,lij->liq", interp_lon, fine_grad, precision=HIGHEST)
    coarse_pad = jnp.einsum("ip,liq->lpq", interp_lat, pulled, precision=HIGHEST) * keeping
    outgoing = []
    for lat_step, lon_step in DIRECTIONS:
        holder = jnp.zeros((levels, lat_rows, lon_cols), jnp.float32)
        holder = holder.at[:, own_cells(lat_step, lat_rows), own_cells(lon_step, lon_cols)].set(
            coarse_pad[:, rim_region(lat_step, lat_rows), rim_region(lon_step, lon_cols)]
        )
        outgoing.append(holder)
    bundle = jnp.stack(outgoing, axis=0)
    incoming = extended(bundle, (("lat", 2), ("lon", 3)), 1)
    coarse_grad = coarse_pad[:, 1:-1, 1:-1]
    for number, (lat_step, lon_step) in enumerate(DIRECTIONS):
        coarse_grad = coarse_grad.at[
            :, own_cells(-lat_step, lat_rows), own_cells(-lon_step, lon_cols)
        ].add(incoming[number][:, rim_region(-lat_step, lat_rows), rim_region(-lon_step, lon_cols)])
    weights_here = slot_pert.astype(jnp.float32)
    share_grad = summed_on_arrival(weights_here * coarse_grad[None], "tm", 0)
    adjoint_mine = spread_field(share_grad, lat_matrix.T, lon_matrix.T)
    return control + gathered_copies(adjoint_mine, "tm", 0)


def solution(mesh):
    placed = (
        P(None, None, "lat", "lon"),
        P("tm", None, None, "lat", "lon"),
        P(),
        P(),
        P("lat", None),
        P("lon", None),
        P("tm", None, "lat", "lon", None),
        P("tm", None, "lat", "lon"),
        P("tm", None, "lat", "lon", None),
        P("tm", None, "lat", "lon", None),
    )
    return jax.shard_map(
        per_device,
        mesh=mesh,
        in_specs=placed,
        out_specs=P(None, None, "lat", "lon"),
        check_vma=False,
    )
```

profile of v0, /device:TPU:1, one launch (start us, length us, event | category | flops | bytes accessed | tf_op | source)
XLA Modules:
  0.0 253.3 jit_solution(16399280534775443478)
XLA Ops:
  1.7 16.2 %all-to-all-start.1 = ((f32[16,16,128]{2,1,0:T(8,128)}), f32[16,16,128]{2,1,0:T(8,128)S(1)}, u32[]{:S(2)}, u32[]{:S(2)}) async-start(f32[16,16,128]{2,1,0:T(8,128)} %bitcast.8), calls=%async_computation.1 | async-start | bytes 262144 | tf_op jit(solution)/shard_map/all_to_all | solution.py:59
  18.5 11.8 %all-to-all-done.1 = f32[16,16,128]{2,1,0:T(8,128)S(1)} async-done(((f32[16,16,128]{2,1,0:T(8,128)}), f32[16,16,128]{2,1,0:T(8,128)S(1)}, u32[]{:S(2)}, u32[]{:S(2)}) %all-to-all-start.1) | async-done | bytes 131104 | tf_op jit(solution)/shard_map/all_to_all | solution.py:59
  32.3 3.5 %all-to-all-start.2 = ((f32[1,256,128]{2,0,1:T(1,128)}), f32[1,256,128]{2,0,1:T(1,128)S(1)}, u32[]{:S(2)}, u32[]{:S(2)}) async-start(f32[1,256,128]{2,0,1:T(1,128)} %copy.41), calls=%async_computation.2 | async-start | bytes 262144 | tf_op jit(solution)/shard_map/all_to_all | solution.py:62
  37.8 10.6 %all-to-all-done.2 = f32[1,256,128]{2,0,1:T(1,128)S(1)} async-done(((f32[1,256,128]{2,0,1:T(1,128)}), f32[1,256,128]{2,0,1:T(1,128)S(1)}, u32[]{:S(2)}, u32[]{:S(2)}) %all-to-all-start.2) | async-done | bytes 131104 | tf_op jit(solution)/shard_map/all_to_all | solution.py:62
  48.3 7.5 %all-to-all-start = ((f32[8,1,192]{2,1,0:T(1,128)}), f32[8,1,192]{2,1,0:T(1,128)S(1)}, u32[]{:S(2)}, u32[]{:S(2)}) async-start(f32[8,1,192]{2,1,0:T(1,128)} %reshape.699), calls=%async_computation | async-start | bytes 16384 | tf_op jit(solution)/shard_map/all_to_all | solution.py:125
  55.8 14.7 %all_gather.6 = f32[16,16,512]{2,1,0:T(8,128)S(1)} all-gather(f32[16,16,128]{2,1,0:T(8,128)S(1)} %bitcast.96), channel_id=1, replica_groups=mesh['tm'=8,'lat'=16,'lon'=4] {'lon'}, dimensions={2}, use_global_device_ids=true | all-gather | bytes 655360 | tf_op jit(solution)/shard_map/all_gather | solution.py:64
  72.0 5.9 %all-to-all-start.3 = ((f32[8,2,8,16,128]{4,3,2,1,0:T(8,128)}), f32[8,2,8,16,128]{4,3,2,1,0:T(8,128)S(1)}, u32[]{:S(2)}, u32[]{:S(2)}) async-start(f32[8,2,8,16,128]{4,3,2,1,0:T(8,128)} %broadcast_in_dim.12), calls=%async_computation.3 | async-start | bytes 2097152 | tf_op jit(solution)/shard_map/all_to_all | solution.py:12
  80.2 12.7 %all-to-all-done.3 = f32[8,2,8,16,128]{4,3,2,1,0:T(8,128)S(1)} async-done(((f32[8,2,8,16,128]{4,3,2,1,0:T(8,128)}), f32[8,2,8,16,128]{4,3,2,1,0:T(8,128)S(1)}, u32[]{:S(2)}, u32[]{:S(2)}) %all-to-all-start.3) | async-done | bytes 1048608 | tf_op jit(solution)/shard_map/all_to_all | solution.py:12
  95.2 9.1 %collective-permute-start.1 = (f32[8,1,128]{2,1,0:T(1,128)S(1)}, f32[8,1,128]{2,1,0:T(1,128)S(1)}, u32[]{:S(2)}, u32[]{:S(2)}) collective-permute-start(f32[8,1,128]{2,1,0:T(1,128)S(1)} %get-tuple-element.223), channel_id=1, source_target_pairs={{4,0},{8,4},{12,8},{16,12},{20,16},{24,20},{28,24},{32,28},{36,32}... | collective-permute-start | bytes 12296 | tf_op jit(solution)/shard_map/ppermute | solution.py:36
  105.2 3.6 %collective-permute-start.2 = (f32[8,18,1]{2,1,0:T(8,128)S(1)}, f32[8,18,1]{2,1,0:T(8,128)S(1)}, u32[]{:S(2)}, u32[]{:S(2)}) collective-permute-start(f32[8,18,1]{2,1,0:T(8,128)S(1)} %get-tuple-element.220), channel_id=1, source_target_pairs={{0,1},{1,2},{2,3},{3,0},{4,5},{5,6},{6,7},{7,4},{8,9},{9,10},{10,1... | collective-permute-start | bytes 1736 | tf_op jit(solution)/shard_map/ppermute | solution.py:35
  108.8 3.9 %collective-permute-start.3 = (f32[8,18,1]{2,1,0:T(8,128)S(1)}, f32[8,18,1]{2,1,0:T(8,128)S(1)}, u32[]{:S(2)}, u32[]{:S(2)}) collective-permute-start(f32[8,18,1]{2,1,0:T(8,128)S(1)} %get-tuple-element.221), channel_id=1, source_target_pairs={{1,0},{2,1},{3,2},{0,3},{5,4},{6,5},{7,6},{4,7},{9,8},{10,9},{11,1... | collective-permute-start | bytes 1736 | tf_op jit(solution)/shard_map/ppermute | solution.py:36
  112.9 2.5 collective-permute-done.3
  116.5 3.1 %gather_fusion = f32[512]{0:T(512)S(1)} fusion(f32[65536]{0:T(1024)S(1)} %bitcast.92, s32[1024]{0:T(1024)S(1)} %pad_clamp_fusion), kind=kCustom, calls=%fused_computation | custom fusion | bytes 6144 | tf_op jit(solution)/shard_map/gather | solution.py:129
  119.6 3.3 %scatter_custom_fusion = f32[65536]{0:T(1024)S(1)} fusion(s32[512]{0:T(512)S(1)} %bitcast.117, f32[512]{0:T(512)S(1)} %subtract_multiply_fusion, f32[]{:T(128)} %constant.416.clone.1), kind=kCustom, calls=%fused_computation.40 | custom fusion | flops 512 | bytes 262148 | tf_op jit(solution)/shard_map/scatter-add | solution.py:131
  126.6 5.0 %collective-permute-start.4 = (f32[8,8,1,128]{3,1,2,0:T(8,128)S(1)}, f32[8,8,1,128]{3,1,2,0:T(8,128)S(1)}, u32[]{:S(2)}, u32[]{:S(2)}) collective-permute-start(f32[8,8,1,128]{3,1,2,0:T(8,128)S(1)} %get-tuple-element.211), channel_id=1, source_target_pairs={{0,4},{4,8},{8,12},{12,16},{16,20},{20,24},{24,28},{28,32},{32,36}... | collective-permute-start | bytes 98312 | tf_op jit(solution)/shard_map/ppermute | solution.py:35
  131.6 6.3 %collective-permute-start.5 = (f32[8,8,1,128]{3,1,2,0:T(8,128)S(1)}, f32[8,8,1,128]{3,1,2,0:T(8,128)S(1)}, u32[]{:S(2)}, u32[]{:S(2)}) collective-permute-start(f32[8,8,1,128]{3,1,2,0:T(8,128)S(1)} %get-tuple-element.212), channel_id=1, source_target_pairs={{4,0},{8,4},{12,8},{16,12},{20,16},{24,20},{28,24},{32,28},{36,32}... | collective-permute-start | bytes 98312 | tf_op jit(solution)/shard_map/ppermute | solution.py:36
  137.9 2.9 %collective-permute-done.5 = f32[8,8,1,128]{3,1,2,0:T(8,128)S(1)} collective-permute-done((f32[8,8,1,128]{3,1,2,0:T(8,128)S(1)}, f32[8,8,1,128]{3,1,2,0:T(8,128)S(1)}, u32[]{:S(2)}, u32[]{:S(2)}) %collective-permute-start.5) | collective-permute-done | bytes 32800 | tf_op jit(solution)/shard_map/ppermute | solution.py:36
  141.6 3.2 %collective-permute-start.6 = (f32[8,8,18,1]{2,1,3,0:T(8,128)S(1)}, f32[8,8,18,1]{2,1,3,0:T(8,128)S(1)}, u32[]{:S(2)}, u32[]{:S(2)}) collective-permute-start(f32[8,8,18,1]{2,1,3,0:T(8,128)S(1)} %copy.52), channel_id=1, source_target_pairs={{0,1},{1,2},{2,3},{3,0},{4,5},{5,6},{6,7},{7,4},{8,9},{9,10},{10,1... | collective-permute-start | bytes 13832 | tf_op jit(solution)/shard_map/ppermute | solution.py:35
  145.3 4.0 %collective-permute-start.7 = (f32[8,8,18,1]{2,1,3,0:T(8,128)S(1)}, f32[8,8,18,1]{2,1,3,0:T(8,128)S(1)}, u32[]{:S(2)}, u32[]{:S(2)}) collective-permute-start(f32[8,8,18,1]{2,1,3,0:T(8,128)S(1)} %copy.53), channel_id=1, source_target_pairs={{1,0},{2,1},{3,2},{0,3},{5,4},{6,5},{7,6},{4,7},{9,8},{10,9},{11,1... | collective-permute-start | bytes 13832 | tf_op jit(solution)/shard_map/ppermute | solution.py:36
  156.8 22.6 %all_to_all.66 = f32[8,2,8,16,128]{4,3,2,1,0:T(8,128)S(1)} all-to-all(f32[8,2,8,16,128]{4,3,2,1,0:T(8,128)S(1)} %convert_multiply_fusion), channel_id=1, replica_groups=mesh['tm'=8,'lat'=16,'lon'=4] {'tm'}, dimensions={0} | all-to-all | bytes 2097152 | tf_op jit(solution)/shard_map/all_to_all | solution.py:48
  179.5 19.1 %all_to_all.67 = f32[16,16,128]{2,1,0:T(8,128)S(1)} all-to-all(f32[16,16,128]{2,1,0:T(8,128)S(1)} %bitcast.98), channel_id=1, replica_groups=mesh['tm'=8,'lat'=16,'lon'=4] {'lat'}, dimensions={0} | all-to-all | bytes 262144 | tf_op jit(solution)/shard_map/all_to_all | solution.py:59
  199.0 15.1 %all_to_all.68 = f32[1,256,128]{2,0,1:T(1,128)S(1)} all-to-all(f32[1,256,128]{2,0,1:T(1,128)S(1)} %copy.57), channel_id=1, replica_groups=mesh['tm'=8,'lat'=16,'lon'=4] {'lat'}, dimensions={1} | all-to-all | bytes 262144 | tf_op jit(solution)/shard_map/all_to_all | solution.py:62
  214.1 13.8 %all_gather.7 = f32[16,16,512]{2,1,0:T(8,128)S(1)} all-gather(f32[16,16,128]{2,1,0:T(8,128)S(1)} %bitcast.100), channel_id=1, replica_groups=mesh['tm'=8,'lat'=16,'lon'=4] {'lon'}, dimensions={2}, use_global_device_ids=true | all-gather | bytes 655360 | tf_op jit(solution)/shard_map/all_gather | solution.py:64
  228.4 23.7 %all_to_all.69 = f32[8,2,8,16,128]{4,3,2,1,0:T(8,128)S(1)} all-to-all(f32[8,2,8,16,128]{4,3,2,1,0:T(8,128)S(1)} %broadcast_in_dim.27), channel_id=1, replica_groups=mesh['tm'=8,'lat'=16,'lon'=4] {'tm'}, dimensions={0} | all-to-all | bytes 2097152 | tf_op jit(solution)/shard_map/all_to_all | solution.py:12
  (114 shorter events, 28.5 us)
Async XLA Ops:
  0.0 70.5 %copy-start = (bf16[512,512]{1,0:T(8,128)(2,1)S(1)}, bf16[512,512]{1,0:T(8,128)(2,1)}, u32[]{:S(2)}) copy-start(bf16[512,512]{1,0:T(8,128)(2,1)} %param.45) | copy-start | bytes 1572868
  0.0 35.8 %copy-start.6 = (f32[1,8,1,1,64]{4,3,2,1,0:T(1,128)S(1)}, f32[1,8,1,1,64]{4,3,2,1,0:T(1,128)}, u32[]{:S(2)}) copy-start(f32[1,8,1,1,64]{4,3,2,1,0:T(1,128)} %param.51) | copy-start | bytes 6148
  0.0 35.8 %copy-start.8 = (s32[1,8,1,1]{1,3,2,0:T(1,128)S(1)}, s32[1,8,1,1]{1,3,2,0:T(1,128)}, u32[]{:S(2)}) copy-start(s32[1,8,1,1]{1,3,2,0:T(1,128)} %param.49) | copy-start | bytes 100
  0.0 35.9 %copy-start.7 = (f32[1,8,1,1,64]{4,3,2,1,0:T(1,128)S(1)}, f32[1,8,1,1,64]{4,3,2,1,0:T(1,128)}, u32[]{:S(2)}) copy-start(f32[1,8,1,1,64]{4,3,2,1,0:T(1,128)} %param.50) | copy-start | bytes 6148
  1.7 28.7 %all-to-all-start.1 = ((f32[16,16,128]{2,1,0:T(8,128)}), f32[16,16,128]{2,1,0:T(8,128)S(1)}, u32[]{:S(2)}, u32[]{:S(2)}) async-start(f32[16,16,128]{2,1,0:T(8,128)} %bitcast.8), calls=%async_computation.1 | async-start | bytes 262144 | tf_op jit(solution)/shard_map/all_to_all | solution.py:59
  32.3 16.1 %all-to-all-start.2 = ((f32[1,256,128]{2,0,1:T(1,128)}), f32[1,256,128]{2,0,1:T(1,128)S(1)}, u32[]{:S(2)}, u32[]{:S(2)}) async-start(f32[1,256,128]{2,0,1:T(1,128)} %copy.41), calls=%async_computation.2 | async-start | bytes 262144 | tf_op jit(solution)/shard_map/all_to_all | solution.py:62
  48.3 22.6 %all-to-all-start = ((f32[8,1,192]{2,1,0:T(1,128)}), f32[8,1,192]{2,1,0:T(1,128)S(1)}, u32[]{:S(2)}, u32[]{:S(2)}) async-start(f32[8,1,192]{2,1,0:T(1,128)} %reshape.699), calls=%async_computation | async-start | bytes 16384 | tf_op jit(solution)/shard_map/all_to_all | solution.py:125
  72.0 6.5 %copy-start.9 = (s32[3]{0:T(128)S(1)}, s32[3]{0:T(128)}, u32[]{:S(2)}) copy-start(s32[3]{0:T(128)} %constant.432.clone.1) | copy-start | bytes 40
  72.0 20.9 %copy-start.1 = (bf16[1,16,8,16,128]{4,3,2,1,0:T(8,128)(2,1)S(1)}, bf16[1,16,8,16,128]{4,3,2,1,0:T(8,128)(2,1)}, u32[]{:S(2)}) copy-start(bf16[1,16,8,16,128]{4,3,2,1,0:T(8,128)(2,1)} %param.43) | copy-start | bytes 1572868
  72.0 20.9 %all-to-all-start.3 = ((f32[8,2,8,16,128]{4,3,2,1,0:T(8,128)}), f32[8,2,8,16,128]{4,3,2,1,0:T(8,128)S(1)}, u32[]{:S(2)}, u32[]{:S(2)}) async-start(f32[8,2,8,16,128]{4,3,2,1,0:T(8,128)} %broadcast_in_dim.12), calls=%async_computation.3 | async-start | bytes 2097152 | tf_op jit(solution)/shard_map/all_to_all | solution.py:12
  77.9 37.5 %copy-start.5 = (f32[32,18]{0,1:T(8,128)S(1)}, f32[32,18]{0,1:T(8,128)}, u32[]{:S(2)}) copy-start(f32[32,18]{0,1:T(8,128)} %param.46) | copy-start | bytes 6916
  92.9 23.1 %copy-start.3 = (f32[256,130]{0,1:T(8,128)S(1)}, f32[256,130]{0,1:T(8,128)}, u32[]{:S(2)}) copy-start(f32[256,130]{0,1:T(8,128)} %param.47) | copy-start | bytes 399364
  93.0 11.4 %collective-permute-start = (f32[8,1,128]{2,1,0:T(1,128)S(1)}, f32[8,1,128]{2,1,0:T(1,128)S(1)}, u32[]{:S(2)}, u32[]{:S(2)}) collective-permute-start(f32[8,1,128]{2,1,0:T(1,128)S(1)} %get-tuple-element.222), channel_id=1, source_target_pairs={{0,4},{4,8},{8,12},{12,16},{16,20},{20,24},{24,28},{28,32},{32,36}... | collective-permute-start | bytes 12296 | tf_op jit(solution)/shard_map/ppermute | solution.py:35
  95.2 9.9 %collective-permute-start.1 = (f32[8,1,128]{2,1,0:T(1,128)S(1)}, f32[8,1,128]{2,1,0:T(1,128)S(1)}, u32[]{:S(2)}, u32[]{:S(2)}) collective-permute-start(f32[8,1,128]{2,1,0:T(1,128)S(1)} %get-tuple-element.223), channel_id=1, source_target_pairs={{4,0},{8,4},{12,8},{16,12},{20,16},{24,20},{28,24},{32,28},{36,32}... | collective-permute-start | bytes 12296 | tf_op jit(solution)/shard_map/ppermute | solution.py:36
  105.2 7.7 %collective-permute-start.2 = (f32[8,18,1]{2,1,0:T(8,128)S(1)}, f32[8,18,1]{2,1,0:T(8,128)S(1)}, u32[]{:S(2)}, u32[]{:S(2)}) collective-permute-start(f32[8,18,1]{2,1,0:T(8,128)S(1)} %get-tuple-element.220), channel_id=1, source_target_pairs={{0,1},{1,2},{2,3},{3,0},{4,5},{5,6},{6,7},{7,4},{8,9},{9,10},{10,1... | collective-permute-start | bytes 1736 | tf_op jit(solution)/shard_map/ppermute | solution.py:35
  108.8 6.6 %collective-permute-start.3 = (f32[8,18,1]{2,1,0:T(8,128)S(1)}, f32[8,18,1]{2,1,0:T(8,128)S(1)}, u32[]{:S(2)}, u32[]{:S(2)}) collective-permute-start(f32[8,18,1]{2,1,0:T(8,128)S(1)} %get-tuple-element.221), channel_id=1, source_target_pairs={{1,0},{2,1},{3,2},{0,3},{5,4},{6,5},{7,6},{4,7},{9,8},{10,9},{11,1... | collective-permute-start | bytes 1736 | tf_op jit(solution)/shard_map/ppermute | solution.py:36
  126.6 11.3 %collective-permute-start.4 = (f32[8,8,1,128]{3,1,2,0:T(8,128)S(1)}, f32[8,8,1,128]{3,1,2,0:T(8,128)S(1)}, u32[]{:S(2)}, u32[]{:S(2)}) collective-permute-start(f32[8,8,1,128]{3,1,2,0:T(8,128)S(1)} %get-tuple-element.211), channel_id=1, source_target_pairs={{0,4},{4,8},{8,12},{12,16},{16,20},{20,24},{24,28},{28,32},{32,36}... | collective-permute-start | bytes 98312 | tf_op jit(solution)/shard_map/ppermute | solution.py:35
  131.6 9.3 %collective-permute-start.5 = (f32[8,8,1,128]{3,1,2,0:T(8,128)S(1)}, f32[8,8,1,128]{3,1,2,0:T(8,128)S(1)}, u32[]{:S(2)}, u32[]{:S(2)}) collective-permute-start(f32[8,8,1,128]{3,1,2,0:T(8,128)S(1)} %get-tuple-element.212), channel_id=1, source_target_pairs={{4,0},{8,4},{12,8},{16,12},{20,16},{24,20},{28,24},{32,28},{36,32}... | collective-permute-start | bytes 98312 | tf_op jit(solution)/shard_map/ppermute | solution.py:36
  141.6 7.8 %collective-permute-start.6 = (f32[8,8,18,1]{2,1,3,0:T(8,128)S(1)}, f32[8,8,18,1]{2,1,3,0:T(8,128)S(1)}, u32[]{:S(2)}, u32[]{:S(2)}) collective-permute-start(f32[8,8,18,1]{2,1,3,0:T(8,128)S(1)} %copy.52), channel_id=1, source_target_pairs={{0,1},{1,2},{2,3},{3,0},{4,5},{5,6},{6,7},{7,4},{8,9},{9,10},{10,1... | collective-permute-start | bytes 13832 | tf_op jit(solution)/shard_map/ppermute | solution.py:35
  145.3 5.2 %collective-permute-start.7 = (f32[8,8,18,1]{2,1,3,0:T(8,128)S(1)}, f32[8,8,18,1]{2,1,3,0:T(8,128)S(1)}, u32[]{:S(2)}, u32[]{:S(2)}) collective-permute-start(f32[8,8,18,1]{2,1,3,0:T(8,128)S(1)} %copy.53), channel_id=1, source_target_pairs={{1,0},{2,1},{3,2},{0,3},{5,4},{6,5},{7,6},{4,7},{9,8},{10,9},{11,1... | collective-permute-start | bytes 13832 | tf_op jit(solution)/shard_map/ppermute | solution.py:36
  179.5 19.2 %copy-start.4 = (bf16[256,256]{1,0:T(8,128)(2,1)S(1)}, bf16[256,256]{1,0:T(8,128)(2,1)}, u32[]{:S(2)}) copy-start(bf16[256,256]{1,0:T(8,128)(2,1)} %param.44) | copy-start | bytes 393220
  228.4 23.7 %copy-start.2 = (f32[16,8,16,128]{3,2,1,0:T(8,128)S(1)}, f32[16,8,16,128]{3,2,1,0:T(8,128)}, u32[]{:S(2)}) copy-start(f32[16,8,16,128]{3,2,1,0:T(8,128)} %param.42) | copy-start | bytes 3145732
where the time goes:
time: 254 us; the launch traced here: 253 us
  blocking collectives  109 us (43%)
  starting transfers between devices  70.4 us (28%)
  waiting for transfers between devices  41.7 us (16%)
  local copies, waits for them, and re-layouts  16.5 us (6%)
  other arithmetic  11.2 us (4%)
  matrix products  3.85 us (2%)
    all_gather x2, blocking collectives, spread_field(): portion = lax.all_gather(halfway, 'lon', axis=2, tiled=True)  28.5 us
    all_to_all x1, blocking collectives, sent_to_all(): lax.all_to_all(jnp.broadcast_to(array[None], (size, *array.shape)), axis,...  23.7 us
    ppermute x4, starting transfers between devices, extended(): after = lax.ppermute(first, axis, down)  23.4 us
    all_to_all x1, blocking collectives, summed_on_arrival(): blocks = lax.all_to_all(split_up(array, dim, size), axis, 0, 0, tiled=True)  22.6 us
    all_to_all x1, blocking collectives, spread_field(): lax.all_to_all(stacked, 'lat', split_axis=0, concat_axis=1, tiled=True)  19.1 us
    all_to_all x1, starting transfers between devices, spread_field(): lax.all_to_all(stacked, 'lat', split_axis=0, concat_axis=1, tiled=True)  16.2 us
    all_to_all x1, blocking collectives, spread_field(): lax.all_to_all(across, 'lat', split_axis=1, concat_axis=0, tiled=True)  15.1 us
    ppermute x4, starting transfers between devices, extended(): before = lax.ppermute(last, axis, up)  13.9 us
  transfers between devices with their start and end apart: 12, of which 7 were waited for; matrix products, arithmetic and copies ran while one was open for 3% of the time, Pallas kernels for 0%

commit v1 on v0

v1 whole, which is shorter than its diff:
```python
import functools

import jax
import jax.numpy as jnp
from jax import lax
from jax.experimental import pallas as pl
from jax.experimental.pallas import tpu as pltpu
from jax.sharding import PartitionSpec as P

F32 = jnp.float32
BF16 = jnp.bfloat16
HIGHEST = lax.Precision.HIGHEST
MESH = pl.DeviceIdType.MESH
ROWS, COLS = 16, 128
FINE_ROWS, FINE_COLS = 32, 256
KR = 256


def halves(x):
    high = x.astype(BF16)
    return high, (x - high.astype(F32)).astype(BF16)


def nt(a, b, **kw):
    return lax.dot_general(a, b, (((1,), (1,)), ((), ())), preferred_element_type=F32, **kw)


def nn(a, b, **kw):
    return lax.dot_general(a, b, (((1,), (0,)), ((), ())), preferred_element_type=F32, **kw)


def kernel(
    NT,
    NL,
    ctl,
    pert,
    latf,
    lonf,
    ilat,
    ilon,
    opk,
    out,
    cs,
    pv,
    lf,
    nf,
    abuf,
    obuf,
    psend,
    pbuf,
    ybuf,
    bbuf,
    inc,
    rows,
    wown,
    woth,
    lr,
    wbuf,
    rtb,
    ctb,
    gb,
    grow,
    gown,
    goth,
    glr,
    hbuf,
    b2,
    adb,
    ap,
    lsem,
    ssem,
    rsem,
):
    t, i, j = lax.axis_index("tm"), lax.axis_index("lat"), lax.axis_index("lon")
    ch = j // 2
    rg = j % 2

    def send(src, dst, phase, where):
        pltpu.make_async_remote_copy(
            src_ref=src,
            dst_ref=dst,
            send_sem=ssem.at[phase],
            recv_sem=rsem.at[phase],
            device_id=where,
            device_id_type=MESH,
        ).start()

    def arrived(ref, phase):
        pltpu.make_async_copy(ref, ref, rsem.at[phase]).wait()

    def sent(ref, phase):
        pltpu.make_async_copy(ref, ref, ssem.at[phase]).wait()

    def loop(first, last, body):
        def step(k, carry):
            body(k)
            return carry

        lax.fori_loop(first, last, step, 0)

    c1 = pltpu.make_async_copy(ctl.at[:, t], cs, lsem.at[0])
    c2 = pltpu.make_async_copy(pert, pv, lsem.at[1])
    c3 = pltpu.make_async_copy(latf, lf, lsem.at[2])
    c4 = pltpu.make_async_copy(lonf.at[pl.ds(ch * 256, 256)], nf, lsem.at[3])
    c1.start()
    c2.start()
    c3.start()
    c4.start()
    c1.wait()

    def send_a(k):
        to = (i + k) % NL
        send(cs.at[to], abuf.at[i], 0, (t, to, j))

    loop(1, NL, send_a)
    abuf[i] = cs[i]

    def send_o(k):
        to = (t + k) % NT
        send(opk.at[to], obuf.at[t], 1, (to, i, j))

    loop(1, NT, send_o)
    obuf[t] = opk[t]

    c2.wait()

    def widen(l):
        x = pv[:, l].astype(F32)
        psend[l * 2] = x[:, :8]
        psend[l * 2 + 1] = x[:, 8:]

    loop(0, NT, widen)

    def send_p(k):
        to = (t + k // 2) % NT
        half = (rg + k) % 2
        send(psend.at[to * 2 + half], pbuf.at[t * 2 + rg], 2, (to, i, ch * 2 + half))

    loop(1, 2 * NT, send_p)
    pbuf[t * 2 + rg] = psend[t * 2 + rg]

    @pl.when(i == 0)
    def _():
        lr[: 4 * NT] = jnp.zeros((4 * NT, 1, COLS), F32)

    @pl.when(i == NL - 1)
    def _():
        lr[4 * NT :] = jnp.zeros((4 * NT, 1, COLS), F32)

    no_rim = jnp.logical_or(
        jnp.logical_and(rg == 0, i == 0), jnp.logical_and(rg == 1, i == NL - 1)
    )
    rim = jnp.logical_not(no_rim)

    @pl.when(no_rim)
    def _():
        glr[...] = jnp.zeros(glr.shape, F32)

    wbuf[...] = jnp.zeros(wbuf.shape, F32)

    k_row = lax.broadcasted_iota(jnp.int32, (KR, 18), 0)
    k_col = lax.broadcasted_iota(jnp.int32, (KR, 18), 1)
    inner = NT * 16
    place = jnp.where(
        k_row < inner,
        1 + (k_row & 15),
        jnp.where(k_row < inner + NT, 0, jnp.where(k_row < inner + 2 * NT, ROWS + 1, -1)),
    )
    pick = (place == k_col).astype(F32)
    p_rows = nt(pick, ilat[...], precision=HIGHEST)
    q_row = lax.broadcasted_iota(jnp.int32, (256, COLS + 2), 0)
    q_col = lax.broadcasted_iota(jnp.int32, (256, COLS + 2), 1)
    place = jnp.where(
        q_row < COLS, q_row + 1, jnp.where(q_row == 255, 0, jnp.where(q_row == COLS, COLS + 1, -1))
    )
    pick = (place == q_col).astype(F32)
    q_rows = nt(pick, ilon[...], precision=HIGHEST)
    arrived(obuf.at[pl.ds(0, NT - 1)], 1)
    lists = jnp.concatenate(
        [obuf[2 * k] + pltpu.roll(obuf[2 * k + 1], 64, 1) for k in range(NT // 2)], axis=1
    )
    n_obs = NT * 64
    cell = lists[0:1].astype(jnp.int32)
    target = lists[1:2]
    weight = lists[2:3]
    o_lev = cell >> 13
    o_row = (cell >> 8) & 31
    o_col = cell & 255
    hot_row = (lax.broadcasted_iota(jnp.int32, (FINE_ROWS, n_obs), 0) == o_row).astype(F32)
    hot_col = (lax.broadcasted_iota(jnp.int32, (FINE_COLS, n_obs), 0) == o_col).astype(F32)
    lev = lax.broadcasted_iota(jnp.int32, (KR, n_obs), 0)
    lev = jnp.where(lev < inner, lev >> 4, jnp.where(lev < inner + NT, lev - inner, lev - inner - NT))
    r_mat = nn(p_rows, hot_row, precision=HIGHEST)
    rtb[...] = jnp.where(lev == o_lev, r_mat, 0.0)
    ctb[...] = nn(q_rows, hot_col, precision=HIGHEST)

    c3.wait()
    c4.wait()
    lat_m = lf[...]
    lat_t = lat_m.astype(F32).T.astype(BF16)
    arrived(abuf.at[pl.ds(0, NL - 1)], 0)
    high, low = halves(abuf[...].reshape(NL * ROWS, COLS))
    both = nn(lat_m, jnp.concatenate([high, low], axis=1))
    ybuf[...] = (both[:, :COLS] + both[:, COLS:]).reshape(2 * NL, 8, COLS)

    def send_b(k):
        lat = (i + k // 4) % NL
        lon = (j + k) % 4
        send(ybuf.at[lat * 2 + lon % 2], bbuf.at[j * NL + i], 3, (t, lat, lon))

    loop(1, 4 * NL, send_b)
    bbuf[j * NL + i] = ybuf[i * 2 + rg]
    arrived(bbuf.at[pl.ds(0, 4 * NL - 1)], 3)

    m8 = NL * 8
    wide = jnp.concatenate(
        [bbuf[NL * b : NL * b + NL].reshape(m8, COLS) for b in range(4)], axis=1
    )
    lon_m = nf[...]
    both = nt(jnp.concatenate(halves(wide), axis=0), lon_m)
    z = both[:m8] + both[m8:]
    z0 = z[:, :COLS].reshape(NL, 8, COLS)
    z1 = z[:, COLS:].reshape(NL, 8, COLS)

    arrived(pbuf.at[pl.ds(0, 2 * NT - 1)], 2)

    for s in range(NT):
        for blk, zz in enumerate((z0, z1)):
            x = jnp.sum(zz * pbuf[2 * s + blk], axis=0)
            inc[2 * s + blk] = x
            rows[2 * s + blk] = jnp.where(rg == 0, x[0:1], x[7:8])

    def send_d(k):
        s = (t + k // 2) % NT
        lon = ch * 2 + (rg + k) % 2
        send(inc.at[pl.ds(2 * s, 2)], wown.at[pl.ds((t * 2 + rg) * 2, 2)], 4, (s, i, lon))

    loop(1, 2 * NT, send_d)

    def send_e(k):
        s = (t + k // 2) % NT
        e = k % 2
        send(inc.at[2 * s + 1 - e], woth.at[t * 2 + rg], 5, (s, i, 2 - 2 * ch + e))

    loop(0, 2 * NT, send_e)

    @pl.when(rim)
    def _():
        lat = i + 2 * rg - 1

        def send_f(k):
            s = (t + k // 4) % NT
            spot = ((1 - rg) * NT + t) * 4 + ch * 2
            send(rows.at[pl.ds(2 * s, 2)], lr.at[pl.ds(spot, 2)], 6 + rg, (s, lat, k % 4))

        loop(0, 4 * NT, send_f)

    wown[(t * 2 + rg) * 2] = inc[2 * t]
    wown[(t * 2 + rg) * 2 + 1] = inc[2 * t + 1]

    arrived(wown.at[pl.ds(0, 2 * (2 * NT - 1))], 4)
    arrived(woth, 5)

    @pl.when(i > 0)
    def _():
        arrived(lr.at[pl.ds(0, 4 * NT)], 7)

    @pl.when(i < NL - 1)
    def _():
        arrived(lr.at[pl.ds(4 * NT, 4 * NT)], 6)

    even = rg == 0
    w = wown[...].reshape(2 * NT, 2, 8, COLS)
    w0, w1 = w[:, 0].reshape(16 * NT, COLS), w[:, 1].reshape(16 * NT, COLS)
    lane = lax.broadcasted_iota(jnp.int32, (16 * NT, COLS), 1)
    near = jnp.where(even, 0, COLS - 1)
    far = COLS - 1 - near
    wbuf[:inner, :COLS] = jnp.where(even, w0, w1)
    wbuf[:inner, COLS:] = jnp.where(
        lane == near,
        jnp.where(even, w1, w0),
        jnp.where(lane == far, woth[...].reshape(16 * NT, COLS), 0.0),
    )
    lane1 = lax.broadcasted_iota(jnp.int32, (1, COLS), 1)
    for k in range(2 * NT):
        before = lr[k * 4 + (j + 3) % 4]
        after = lr[k * 4 + (j + 1) % 4]
        wbuf[inner + k : inner + k + 1, :COLS] = lr[k * 4 + j]
        wbuf[inner + k : inner + k + 1, COLS:] = jnp.where(
            lane1 == COLS - 1, before, jnp.where(lane1 == 0, after, 0.0)
        )

    r_high, r_low = halves(rtb[...])
    w_high, w_low = halves(wbuf[...].T)
    both = nn(jnp.concatenate([w_high, w_low], axis=0), r_high)
    mixed = both[:256] + both[256:] + nn(w_high, r_low)
    cols = ctb[...]
    seen = jnp.sum(mixed * cols, axis=0, keepdims=True)
    departure = weight * (seen - target)
    d_high, d_low = halves(cols * departure)
    both = nt(jnp.concatenate([r_high, r_low], axis=0), d_high)
    g = both[:KR] + both[KR:] + nt(r_high, d_low)
    for k in range(2 * NT):
        gb[2 * k] = g[8 * k : 8 * k + 8, :COLS]
        gb[2 * k + 1] = g[8 * k : 8 * k + 8, COLS:]
    for k in range(2 * NT):
        grow[2 * k] = g[inner + k : inner + k + 1, :COLS]
        grow[2 * k + 1] = g[inner + k : inner + k + 1, COLS:]

    def send_g(k):
        l = (t + k // 2) % NT
        half = (rg + k) % 2
        send(
            gb.at[pl.ds((l * 2 + half) * 2, 2)],
            gown.at[pl.ds((t * 2 + rg) * 2, 2)],
            8,
            (l, i, ch * 2 + half),
        )

    loop(1, 2 * NT, send_g)

    def send_h(k):
        l = (t + k // 2) % NT
        half = k % 2
        send(
            gb.at[(l * 2 + half) * 2 + 1], goth.at[t * 2 + rg], 9, (l, i, 2 - 2 * ch + half)
        )

    loop(0, 2 * NT, send_h)

    def send_rim(pos):
        def go(k):
            l = (t + k // 2) % NT
            send(
                grow.at[pl.ds((pos * NT + l) * 2, 2)],
                glr.at[pl.ds((t * 4 + j) * 2, 2)],
                10 + pos,
                (l, i - 1 + 2 * pos, (k % 2) * 2 + 1 - pos),
            )

        loop(0, 2 * NT, go)

    @pl.when(i > 0)
    def _():
        send_rim(0)

    @pl.when(i < NL - 1)
    def _():
        send_rim(1)

    gown[(t * 2 + rg) * 2] = gb[(t * 2 + rg) * 2]
    gown[(t * 2 + rg) * 2 + 1] = gb[(t * 2 + rg) * 2 + 1]
    arrived(gown.at[pl.ds(0, 2 * (2 * NT - 1))], 8)
    arrived(goth, 9)

    @pl.when(jnp.logical_and(rim, rg == 1))
    def _():
        arrived(glr, 10)

    @pl.when(jnp.logical_and(rim, rg == 0))
    def _():
        arrived(glr, 11)

    lane8 = lax.broadcasted_iota(jnp.int32, (8, COLS), 1)
    row8 = lax.broadcasted_iota(jnp.int32, (8, COLS), 0)
    first, last = lane8 == 0, lane8 == COLS - 1
    mine = row8 == jnp.where(even, 0, 7)
    other = 2 - 2 * ch
    acc0 = acc1 = None
    for s in range(NT):
        def rim_of(b, part, s=s):
            return jnp.broadcast_to(glr[(s * 4 + b) * 2 + part], (8, COLS))

        d0 = gown[s * 4] + jnp.where(last, gown[s * 4 + 3], 0.0)
        d0 = d0 + jnp.where(first, goth[s * 2 + 1], 0.0)
        e0 = rim_of(ch * 2, 0) + jnp.where(last, rim_of(ch * 2 + 1, 1), 0.0)
        e0 = e0 + jnp.where(first, rim_of(other + 1, 1), 0.0)
        d0 = d0 + jnp.where(mine, e0, 0.0)
        d1 = gown[s * 4 + 2] + jnp.where(first, gown[s * 4 + 1], 0.0)
        d1 = d1 + jnp.where(last, goth[s * 2], 0.0)
        e1 = rim_of(ch * 2 + 1, 0) + jnp.where(first, rim_of(ch * 2, 1), 0.0)
        e1 = e1 + jnp.where(last, rim_of(other, 1), 0.0)
        d1 = d1 + jnp.where(mine, e1, 0.0)
        p0, p1 = pbuf[2 * s] * d0[None], pbuf[2 * s + 1] * d1[None]
        acc0, acc1 = (p0, p1) if s == 0 else (acc0 + p0, acc1 + p1)
    grad = jnp.concatenate([acc0.reshape(m8, COLS), acc1.reshape(m8, COLS)], axis=1)
    both = nn(jnp.concatenate(halves(grad), axis=0), lon_m)
    h = both[:m8] + both[m8:]
    for b in range(4):
        hbuf[NL * b : NL * b + NL] = h[:, b * COLS : (b + 1) * COLS].reshape(NL, 8, COLS)

    def send_c(k):
        lat = (i + k // 4) % NL
        lon = (j + k) % 4
        send(hbuf.at[lon * NL + lat], b2.at[ch * 2 * NL + 2 * i + rg], 12, (t, lat, lon))

    loop(1, 4 * NL, send_c)
    b2[ch * 2 * NL + 2 * i + rg] = hbuf[j * NL + i]
    arrived(b2.at[pl.ds(0, 4 * NL - 1)], 12)
    y = (b2[: 2 * NL] + b2[2 * NL :]).reshape(NL * ROWS, COLS)
    high, low = halves(y)
    both = nn(lat_t, jnp.concatenate([high, low], axis=1))
    adb[...] = (both[:, :COLS] + both[:, COLS:]).reshape(NL, ROWS, COLS)

    def send_i(k):
        to = (i + k) % NL
        send(adb.at[to], ap.at[i], 13, (t, to, j))

    loop(1, NL, send_i)
    ap[i] = adb[i]
    arrived(ap.at[pl.ds(0, NL - 1)], 13)

    def send_j(k):
        send(ap, out.at[:, t], 14, ((t + k) % NT, i, j))

    loop(1, NT, send_j)
    last_copy = pltpu.make_async_copy(ap, out.at[:, t], lsem.at[0])
    last_copy.start()
    last_copy.wait()
    arrived(out.at[:, pl.ds(0, NT - 1)], 14)

    sent(abuf.at[pl.ds(0, NL - 1)], 0)
    sent(obuf.at[pl.ds(0, NT - 1)], 1)
    sent(pbuf.at[pl.ds(0, 2 * NT - 1)], 2)
    sent(bbuf.at[pl.ds(0, 4 * NL - 1)], 3)
    sent(wown.at[pl.ds(0, 2 * (2 * NT - 1))], 4)
    sent(woth, 5)

    @pl.when(jnp.logical_and(rim, rg == 0))
    def _():
        sent(glr, 6)

    @pl.when(jnp.logical_and(rim, rg == 1))
    def _():
        sent(glr, 7)

    sent(gown.at[pl.ds(0, 2 * (2 * NT - 1))], 8)
    sent(goth, 9)

    @pl.when(i > 0)
    def _():
        sent(lr.at[pl.ds(0, 4 * NT)], 10)

    @pl.when(i < NL - 1)
    def _():
        sent(lr.at[pl.ds(0, 4 * NT)], 11)

    sent(b2.at[pl.ds(0, 4 * NL - 1)], 12)
    sent(ap.at[pl.ds(0, NL - 1)], 13)
    sent(out.at[:, pl.ds(0, NT - 1)], 14)


def per_device(NT, NL, control, pert, latf, lonf, ilat, ilon, cell, count, value, weight):
    cap = cell.shape[-1]
    usable = (jnp.arange(cap) < count[0, :, 0, 0, None]).astype(F32)
    lists = jnp.stack(
        [cell[0, :, 0, 0].astype(F32), value[0, :, 0, 0], weight[0, :, 0, 0] * usable], axis=1
    )
    lists = jnp.pad(lists, ((0, 0), (0, 5), (0, COLS - cap)))
    any_space = pl.BlockSpec(memory_space=pl.ANY)
    vmem = pl.BlockSpec(memory_space=pltpu.VMEM)
    V = pltpu.VMEM
    tile = (8, COLS)
    scratch = [
        V((NL, ROWS, COLS), F32),
        V((NL, NT, ROWS, COLS), BF16),
        V((NL * ROWS, NL * ROWS), BF16),
        V((256, 512), BF16),
        V((NL, ROWS, COLS), F32),
        V((NT, *tile), F32),
        V((2 * NT, NL, *tile), F32),
        V((2 * NT, NL, *tile), F32),
        V((2 * NL, *tile), F32),
        V((4 * NL, *tile), F32),
        V((2 * NT, *tile), F32),
        V((2 * NT, 1, COLS), F32),
        V((4 * NT, *tile), F32),
        V((2 * NT, *tile), F32),
        V((8 * NT, 1, COLS), F32),
        V((KR, 256), F32),
        V((KR, NT * 64), F32),
        V((256, NT * 64), F32),
        V((4 * NT, *tile), F32),
        V((4 * NT, 1, COLS), F32),
        V((4 * NT, *tile), F32),
        V((2 * NT, *tile), F32),
        V((8 * NT, 1, COLS), F32),
        V((4 * NL, *tile), F32),
        V((4 * NL, *tile), F32),
        V((NL, ROWS, COLS), F32),
        V((NL, ROWS, COLS), F32),
        pltpu.SemaphoreType.DMA((4,)),
        pltpu.SemaphoreType.DMA((15,)),
        pltpu.SemaphoreType.DMA((15,)),
    ]
    adjoint = pl.pallas_call(
        functools.partial(kernel, NT, NL),
        name="gradient",
        out_shape=jax.ShapeDtypeStruct(control.shape, F32),
        in_specs=[any_space] * 4 + [vmem] * 3,
        out_specs=any_space,
        scratch_shapes=scratch,
        compiler_params=pltpu.CompilerParams(
            has_side_effects=True, vmem_limit_bytes=24 * 1024 * 1024
        ),
    )(control, pert[0], latf, lonf, ilat, ilon, lists)
    return control + adjoint


def solution(mesh):
    placed = (
        P(None, None, "lat", "lon"),
        P("tm", None, None, "lat", "lon"),
        P(),
        P(),
        P("lat", None),
        P("lon", None),
        P("tm", None, "lat", "lon", None),
        P("tm", None, "lat", "lon"),
        P("tm", None, "lat", "lon", None),
        P("tm", None, "lat", "lon", None),
    )
    return jax.shard_map(
        functools.partial(per_device, mesh.shape["tm"], mesh.shape["lat"]),
        mesh=mesh,
        in_specs=placed,
        out_specs=P(None, None, "lat", "lon"),
        check_vma=False,
    )
```

time: 254 us -> 107 us (0.42)
  blocking collectives: 109 us -> 0 us
  Pallas kernels: 0 us -> 99.6 us
  starting transfers between devices: 70.4 us -> 0 us
  waiting for transfers between devices: 41.7 us -> 0 us
  local copies, waits for them, and re-layouts: 16.5 us -> 5.75 us
  other arithmetic: 11.2 us -> 1.21 us
  matrix products: 3.85 us -> 0 us
    pallas_call x0 -> x1, Pallas kernels: none -> 99.6 us  [per_device(): pl.pallas_call(functools.partial(kernel, NT, NL), name='gradient', out_sh...]
    all_to_all x4 -> x0, blocking collectives: 80.5 us -> none  [the longest x1 23.7 us: sent_to_all(): lax.all_to_all(jnp.broadcast_to(array[None], (size, *array.shape)), axis,...]
    ppermute x8 -> x0, starting transfers between devices: 37.3 us -> none  [the longest x4 23.4 us: extended(): after = lax.ppermute(first, axis, down)]
    all_to_all x4 -> x0, waiting for transfers between devices: 35 us -> none  [the longest x1 12.7 us: sent_to_all(): lax.all_to_all(jnp.broadcast_to(array[None], (size, *array.shape)), axis,...]
    all_to_all x4 -> x0, starting transfers between devices: 33.1 us -> none  [the longest x1 16.2 us: spread_field(): lax.all_to_all(stacked, 'lat', split_axis=0, concat_axis=1, tiled=True)]
    all_gather x2 -> x0, blocking collectives: 28.5 us -> none  [spread_field(): portion = lax.all_gather(halfway, 'lon', axis=2, tiled=True)]
    ppermute x8 -> x0, waiting for transfers between devices: 6.69 us -> none  [the longest x4 6.68 us: extended(): after = lax.ppermute(first, axis, down)]
    unnamed x32 -> x20, local copies, waits for them, and re-layouts: 1.6 us -> 5.75 us
  transfers between devices with their start and end apart: 12 -> 0, of which waited for: 7 -> 0; matrix products, arithmetic and copies ran while one was open for 3% -> 0% of each run, Pallas kernels for 0% -> 0%
where the time goes in v1:
time: 107 us
  Pallas kernels  99.6 us (93%)
  local copies, waits for them, and re-layouts  5.75 us (5%)
  other arithmetic  1.21 us (1%)
    pallas_call x1, Pallas kernels, per_device(): pl.pallas_call(functools.partial(kernel, NT, NL), name='gradient', out_sh...  99.6 us
    unnamed x20, local copies, waits for them, and re-layouts  5.75 us

profile of v1, /device:TPU:1, one launch (start us, length us, event | category | flops | bytes accessed | tf_op | source)
XLA Modules:
  0.0 106.6 jit_solution(5255238012154325409)
XLA Ops:
  0.0 0.0 copy-start.5
  0.0 0.0 copy-start.6
  0.0 0.0 copy-start.8
  0.0 0.0 copy-start.4
  0.0 0.7 copy-done.5
  0.7 0.0 copy-done.6
  0.7 0.0 copy-done.8
  0.7 0.1 compare_select_fusion
  0.8 0.0 copy-done.4
  0.8 0.0 copy-start.7
  0.8 0.1 copy.12.ilat
  0.9 0.6 copy-done.7
  1.5 0.0 copy-start.3
  1.5 1.1 %copy.13.ilon = f32[256,130]{1,0:T(8,128)S(1)} copy(f32[256,130]{0,1:T(8,128)} %param.15) | data formatting | bytes 266240 | tf_op args[5]
  2.6 0.0 copy-done.3
  2.6 0.0 copy-start
  2.6 1.2 %copy-done = f32[16,8,16,128]{3,2,1,0:T(8,128)S(1)} copy-done((f32[16,8,16,128]{3,2,1,0:T(8,128)S(1)}, f32[16,8,16,128]{3,2,1,0:T(8,128)}, u32[]{:S(2)}) %copy-start) | copy-done | bytes 1048600
  3.8 0.0 copy-start.1
  3.8 1.0 copy-done.1
  4.9 0.0 copy-start.2
  4.9 1.0 copy-done.2
  5.9 99.6 %gradient.1 = f32[16,8,16,128]{3,2,1,0:T(8,128)S(1)} custom-call(f32[16,8,16,128]{3,2,1,0:T(8,128)S(1)} %copy-done, bf16[16,8,16,128]{3,2,1,0:T(8,128)(2,1)S(1)} %bitcast.7, bf16[256,256]{1,0:T(8,128)(2,1)S(1)} %copy-done.3, bf16[512,512]{1,0:T(8,128)(2,1)S(1)} %copy-done.2, f32[32,18]{1,0:T(8,128)S(1)} %copy.12.ilat, f32[256,130]{1,0:T(8,128)S(1)} %copy.13.ilon, ...), custom_call_target="tpu_custom_call" | custom-call | tf_op jit(solution)/shard_map/gradient/pallas_call | solution.py:496
  105.5 1.1 %add.5 = f32[16,8,16,128]{3,2,1,0:T(8,128)} add(f32[16,8,16,128]{3,2,1,0:T(8,128)S(1)} %copy-done, f32[16,8,16,128]{3,2,1,0:T(8,128)S(1)} %gradient.1) | non-fusion elementwise | flops 262144 | bytes 3145728 | tf_op jit(solution)/shard_map/add | solution.py:507
  (2 shorter events, 0.0 us)
Async XLA Ops:
  0.0 0.7 copy-start.5
  0.0 0.7 copy-start.6
  0.0 0.7 copy-start.8
  0.0 0.8 copy-start.4
  0.8 0.7 copy-start.7
  1.5 1.1 %copy-start.3 = (bf16[256,256]{1,0:T(8,128)(2,1)S(1)}, bf16[256,256]{1,0:T(8,128)(2,1)}, u32[]{:S(2)}) copy-start(bf16[256,256]{1,0:T(8,128)(2,1)} %latf.1) | copy-start | bytes 393220
  2.6 1.2 %copy-start = (f32[16,8,16,128]{3,2,1,0:T(8,128)S(1)}, f32[16,8,16,128]{3,2,1,0:T(8,128)}, u32[]{:S(2)}) copy-start(f32[16,8,16,128]{3,2,1,0:T(8,128)} %ctl.1) | copy-start | bytes 3145732
  3.8 1.0 copy-start.1
  4.9 1.0 copy-start.2

commit v2 on v1

--- a/solution.py
+++ b/solution.py
@@ -38,8 +38,18 @@
     lonf,
     ilat,
     ilon,
+    o_cell,
+    o_count,
+    o_value,
+    o_weight,
+    out,
+    vlat,
+    vlon,
+    vcell,
+    vcount,
+    vvalue,
+    vweight,
     opk,
-    out,
     cs,
     pv,
     lf,
@@ -66,10 +76,10 @@
     hbuf,
     b2,
     adb,
-    ap,
     lsem,
     ssem,
     rsem,
+    hsem,
 ):
     t, i, j = lax.axis_index("tm"), lax.axis_index("lat"), lax.axis_index("lon")
     ch = j // 2
@@ -98,31 +108,55 @@
 
         lax.fori_loop(first, last, step, 0)
 
-    c1 = pltpu.make_async_copy(ctl.at[:, t], cs, lsem.at[0])
-    c2 = pltpu.make_async_copy(pert, pv, lsem.at[1])
-    c3 = pltpu.make_async_copy(latf, lf, lsem.at[2])
-    c4 = pltpu.make_async_copy(lonf.at[pl.ds(ch * 256, 256)], nf, lsem.at[3])
-    c1.start()
-    c2.start()
-    c3.start()
-    c4.start()
-    c1.wait()
-
-    def send_a(k):
-        to = (i + k) % NL
-        send(cs.at[to], abuf.at[i], 0, (t, to, j))
-
-    loop(1, NL, send_a)
-    abuf[i] = cs[i]
-
-    def send_o(k):
-        to = (t + k) % NT
-        send(opk.at[to], obuf.at[t], 1, (to, i, j))
-
-    loop(1, NT, send_o)
-    obuf[t] = opk[t]
-
-    c2.wait()
+    copies = [
+        pltpu.make_async_copy(src, dst, lsem.at[n])
+        for n, (src, dst) in enumerate(
+            (
+                (pert, pv),
+                (ilat, vlat),
+                (ilon, vlon),
+                (o_cell, vcell),
+                (o_count, vcount),
+                (o_value, vvalue),
+                (o_weight, vweight),
+                (ctl.at[:, t], cs),
+                (latf, lf),
+                (lonf.at[pl.ds(ch * 256, 256)], nf),
+            )
+        )
+    ]
+    for copy in copies:
+        copy.start()
+
+    ready = pltpu.get_barrier_semaphore()
+
+    def hello(*where):
+        pl.semaphore_signal(ready, inc=1, device_id=where, device_id_type=MESH)
+
+    loop(1, 4 * NL, lambda k: hello(t, (i + k // 4) % NL, (j + k) % 4))
+    loop(4, 4 * NT, lambda k: hello((t + k // 4) % NT, i, (j + k) % 4))
+
+    @pl.when(i < NL - 1)
+    def _():
+        loop(2, 2 * NT, lambda k: hello((t + k // 2) % NT, i + 1, (k % 2) * 2))
+
+        @pl.when(rg == 1)
+        def _():
+            loop(2, 2 * NT, lambda k: hello((t + k // 2) % NT, i + 1, (k % 2) * 2 + 1))
+
+    @pl.when(i > 0)
+    def _():
+        loop(2, 2 * NT, lambda k: hello((t + k // 2) % NT, i - 1, (k % 2) * 2 + 1))
+
+        @pl.when(rg == 0)
+        def _():
+            loop(2, 2 * NT, lambda k: hello((t + k // 2) % NT, i - 1, (k % 2) * 2))
+
+    peers = 4 * NL - 1 + 4 * NT - 4
+    peers = peers + jnp.where(i < NL - 1, (NT - 1) * (2 + 2 * rg), 0)
+    peers = peers + jnp.where(i > 0, (NT - 1) * (4 - 2 * rg), 0)
+
+    copies[0].wait()
 
     def widen(l):
         x = pv[:, l].astype(F32)
@@ -130,6 +164,53 @@
         psend[l * 2 + 1] = x[:, 8:]
 
     loop(0, NT, widen)
+    for copy in copies[1:7]:
+        copy.wait()
+    opk[...] = jnp.zeros(opk.shape, F32)
+    slot_entry = lax.broadcasted_iota(jnp.int32, (1, 64), 1)
+    for s in range(NT):
+        usable = slot_entry < vcount[0:1, s : s + 1]
+        opk[s, 0:1, :64] = vcell[s].astype(F32)
+        opk[s, 1:2, :64] = vvalue[s]
+        opk[s, 2:3, :64] = jnp.where(usable, vweight[s], 0.0)
+
+    @pl.when(i == 0)
+    def _():
+        lr[: 4 * NT] = jnp.zeros((4 * NT, 1, COLS), F32)
+
+    @pl.when(i == NL - 1)
+    def _():
+        lr[4 * NT :] = jnp.zeros((4 * NT, 1, COLS), F32)
+
+    no_rim = jnp.logical_or(
+        jnp.logical_and(rg == 0, i == 0), jnp.logical_and(rg == 1, i == NL - 1)
+    )
+    rim = jnp.logical_not(no_rim)
+
+    @pl.when(no_rim)
+    def _():
+        glr[...] = jnp.zeros(glr.shape, F32)
+
+    wbuf[...] = jnp.zeros(wbuf.shape, F32)
+    for copy in copies[7:]:
+        copy.wait()
+    lat_m = lf[...]
+    lat_t = lat_m.astype(F32).T.astype(BF16)
+    pl.semaphore_wait(ready, peers)
+
+    def send_a(k):
+        to = (i + k) % NL
+        send(cs.at[to], abuf.at[i], 0, (t, to, j))
+
+    loop(1, NL, send_a)
+    abuf[i] = cs[i]
+
+    def send_o(k):
+        to = (t + k) % NT
+        send(opk.at[to], obuf.at[t], 1, (to, i, j))
+
+    loop(1, NT, send_o)
+    obuf[t] = opk[t]
 
     def send_p(k):
         to = (t + k // 2) % NT
@@ -138,25 +219,6 @@
 
     loop(1, 2 * NT, send_p)
     pbuf[t * 2 + rg] = psend[t * 2 + rg]
-
-    @pl.when(i == 0)
-    def _():
-        lr[: 4 * NT] = jnp.zeros((4 * NT, 1, COLS), F32)
-
-    @pl.when(i == NL - 1)
-    def _():
-        lr[4 * NT :] = jnp.zeros((4 * NT, 1, COLS), F32)
-
-    no_rim = jnp.logical_or(
-        jnp.logical_and(rg == 0, i == 0), jnp.logical_and(rg == 1, i == NL - 1)
-    )
-    rim = jnp.logical_not(no_rim)
-
-    @pl.when(no_rim)
-    def _():
-        glr[...] = jnp.zeros(glr.shape, F32)
-
-    wbuf[...] = jnp.zeros(wbuf.shape, F32)
 
     k_row = lax.broadcasted_iota(jnp.int32, (KR, 18), 0)
     k_col = lax.broadcasted_iota(jnp.int32, (KR, 18), 1)
@@ -167,14 +229,14 @@
         jnp.where(k_row < inner + NT, 0, jnp.where(k_row < inner + 2 * NT, ROWS + 1, -1)),
     )
     pick = (place == k_col).astype(F32)
-    p_rows = nt(pick, ilat[...], precision=HIGHEST)
+    p_rows = nn(pick, vlat[...], precision=HIGHEST)
     q_row = lax.broadcasted_iota(jnp.int32, (256, COLS + 2), 0)
     q_col = lax.broadcasted_iota(jnp.int32, (256, COLS + 2), 1)
     place = jnp.where(
         q_row < COLS, q_row + 1, jnp.where(q_row == 255, 0, jnp.where(q_row == COLS, COLS + 1, -1))
     )
     pick = (place == q_col).astype(F32)
-    q_rows = nt(pick, ilon[...], precision=HIGHEST)
+    q_rows = nn(pick, vlon[...], precision=HIGHEST)
     arrived(obuf.at[pl.ds(0, NT - 1)], 1)
     lists = jnp.concatenate(
         [obuf[2 * k] + pltpu.roll(obuf[2 * k + 1], 64, 1) for k in range(NT // 2)], axis=1
@@ -194,10 +256,6 @@
     rtb[...] = jnp.where(lev == o_lev, r_mat, 0.0)
     ctb[...] = nn(q_rows, hot_col, precision=HIGHEST)
 
-    c3.wait()
-    c4.wait()
-    lat_m = lf[...]
-    lat_t = lat_m.astype(F32).T.astype(BF16)
     arrived(abuf.at[pl.ds(0, NL - 1)], 0)
     high, low = halves(abuf[...].reshape(NL * ROWS, COLS))
     both = nn(lat_m, jnp.concatenate([high, low], axis=1))
@@ -402,22 +460,73 @@
     both = nn(lat_t, jnp.concatenate([high, low], axis=1))
     adb[...] = (both[:, :COLS] + both[:, COLS:]).reshape(NL, ROWS, COLS)
 
+    chunks = 4 if NL % 4 == 0 else NL
+    size = NL // chunks
+    own = i // size
+
     def send_i(k):
         to = (i + k) % NL
-        send(adb.at[to], ap.at[i], 13, (t, to, j))
+        send(adb.at[to], out.at[i, t], 16 + own, (t, to, j))
 
     loop(1, NL, send_i)
-    ap[i] = adb[i]
-    arrived(ap.at[pl.ds(0, NL - 1)], 13)
-
-    def send_j(k):
-        send(ap, out.at[:, t], 14, ((t + k) % NT, i, j))
-
-    loop(1, NT, send_j)
-    last_copy = pltpu.make_async_copy(ap, out.at[:, t], lsem.at[0])
-    last_copy.start()
-    last_copy.wait()
-    arrived(out.at[:, pl.ds(0, NT - 1)], 14)
+    out[i, t] = adb[i]
+
+    core = t % 2
+    sibling = t + 1 - 2 * core
+    right, left = (t + 2) % NT, (t + NT - 2) % NT
+    chips = NT // 2
+    order = (0, 1, 3, 2) if chunks == 4 else tuple(range(chunks))
+    places = [(own + o) % chunks for o in order]
+
+    def chunk(q, owner):
+        return out.at[pl.ds(q * size, size), owner]
+
+    def pass_on(q, owner, n, to):
+        pltpu.make_async_remote_copy(
+            src_ref=chunk(q, owner),
+            dst_ref=chunk(q, owner),
+            send_sem=ssem.at[14],
+            recv_sem=hsem.at[n],
+            device_id=(to, i, j),
+            device_id_type=MESH,
+        ).start()
+
+    def landed(q, n):
+        pltpu.make_async_copy(chunk(q, t), chunk(q, t), hsem.at[n]).wait()
+
+    from_left, from_right, from_far, from_sibling = 0, chunks, 2 * chunks, 3 * chunks
+
+    def relay(k):
+        q = places[k]
+        landed(q, from_left + k)
+        if 2 * k < chunks:
+            pass_on(q, left, from_far + k, right)
+        pass_on(q, left, from_sibling, sibling)
+        landed(q, from_right + k)
+        if 2 * k >= chunks:
+            pass_on(q, right, from_far + k, left)
+        pass_on(q, right, from_sibling, sibling)
+
+    for k, q in enumerate(places):
+        if k == 0:
+            if size > 1:
+                arrived(out.at[pl.ds(0, size - 1), t], 16 + q)
+        else:
+            arrived(out.at[pl.ds(0, size), t], 16 + q)
+        if chips > 1:
+            pass_on(q, t, from_left + k, right)
+            pass_on(q, t, from_right + k, left)
+        pass_on(q, t, from_sibling, sibling)
+        if chips > 1 and k > 0:
+            relay(k - 1)
+    if chips > 1:
+        relay(chunks - 1)
+        across = (t + NT // 2) % NT
+        for k, q in enumerate(places):
+            landed(q, from_far + k)
+            pass_on(q, across, from_sibling, sibling)
+    everything = out.at[:, pl.ds(0, chips)]
+    pltpu.make_async_copy(everything, everything, hsem.at[from_sibling]).wait()
 
     sent(abuf.at[pl.ds(0, NL - 1)], 0)
     sent(obuf.at[pl.ds(0, NT - 1)], 1)
@@ -446,22 +555,23 @@
         sent(lr.at[pl.ds(0, 4 * NT)], 11)
 
     sent(b2.at[pl.ds(0, 4 * NL - 1)], 12)
-    sent(ap.at[pl.ds(0, NL - 1)], 13)
+    sent(out.at[pl.ds(0, NL - 1), t], 16 + own)
     sent(out.at[:, pl.ds(0, NT - 1)], 14)
 
 
 def per_device(NT, NL, control, pert, latf, lonf, ilat, ilon, cell, count, value, weight):
-    cap = cell.shape[-1]
-    usable = (jnp.arange(cap) < count[0, :, 0, 0, None]).astype(F32)
-    lists = jnp.stack(
-        [cell[0, :, 0, 0].astype(F32), value[0, :, 0, 0], weight[0, :, 0, 0] * usable], axis=1
-    )
-    lists = jnp.pad(lists, ((0, 0), (0, 5), (0, COLS - cap)))
-    any_space = pl.BlockSpec(memory_space=pl.ANY)
-    vmem = pl.BlockSpec(memory_space=pltpu.VMEM)
+    hbm = pl.BlockSpec(memory_space=pltpu.HBM)
     V = pltpu.VMEM
     tile = (8, COLS)
+    cap = cell.shape[-1]
     scratch = [
+        V((ROWS + 2, FINE_ROWS), F32),
+        V((COLS + 2, FINE_COLS), F32),
+        V((NT, 1, cap), jnp.int32),
+        V((1, NT), jnp.int32),
+        V((NT, 1, cap), F32),
+        V((NT, 1, cap), F32),
+        V((NT, *tile), F32),
         V((NL, ROWS, COLS), F32),
         V((NL, NT, ROWS, COLS), BF16),
         V((NL * ROWS, NL * ROWS), BF16),
@@ -488,22 +598,33 @@
         V((4 * NL, *tile), F32),
         V((4 * NL, *tile), F32),
         V((NL, ROWS, COLS), F32),
-        V((NL, ROWS, COLS), F32),
-        pltpu.SemaphoreType.DMA((4,)),
-        pltpu.SemaphoreType.DMA((15,)),
-        pltpu.SemaphoreType.DMA((15,)),
+        pltpu.SemaphoreType.DMA((10,)),
+        pltpu.SemaphoreType.DMA((20,)),
+        pltpu.SemaphoreType.DMA((20,)),
+        pltpu.SemaphoreType.DMA((13,)),
     ]
     adjoint = pl.pallas_call(
         functools.partial(kernel, NT, NL),
         name="gradient",
         out_shape=jax.ShapeDtypeStruct(control.shape, F32),
-        in_specs=[any_space] * 4 + [vmem] * 3,
-        out_specs=any_space,
+        in_specs=[hbm] * 10,
+        out_specs=pl.BlockSpec(memory_space=pltpu.VMEM),
         scratch_shapes=scratch,
         compiler_params=pltpu.CompilerParams(
-            has_side_effects=True, vmem_limit_bytes=24 * 1024 * 1024
+            has_side_effects=True, collective_id=0, vmem_limit_bytes=63 * 1024 * 1024
         ),
-    )(control, pert[0], latf, lonf, ilat, ilon, lists)
+    )(
+        control,
+        pert[0],
+        latf,
+        lonf,
+        ilat.T,
+        ilon.T,
+        cell.reshape(NT, 1, cap),
+        count.reshape(1, NT),
+        value.reshape(NT, 1, cap),
+        weight.reshape(NT, 1, cap),
+    )
     return control + adjoint
 
 

time: 107 us -> 94 us (0.88)
  Pallas kernels: 99.6 us -> 91.2 us
  local copies, waits for them, and re-layouts: 5.75 us -> 0 us
  other arithmetic: 1.21 us -> 2.67 us
    pallas_call x1, Pallas kernels: 99.6 us -> 91.2 us  [per_device(): pl.pallas_call(functools.partial(kernel, NT, NL), name='gradient', out_sh...]
    unnamed x20 -> x0, local copies, waits for them, and re-layouts: 5.75 us -> none
    add x1, other arithmetic: 1.11 us -> 2.67 us  [per_device(): return control + adjoint]
where the time goes in v2:
time: 94 us; the launch traced here: 93.9 us
  Pallas kernels  91.2 us (97%)
  other arithmetic  2.67 us (3%)
    pallas_call x1, Pallas kernels, per_device(): pl.pallas_call(functools.partial(kernel, NT, NL), name='gradient', out_sh...  91.2 us
    add x1, other arithmetic, per_device(): return control + adjoint  2.67 us

profile of v2, /device:TPU:1, one launch (start us, length us, event | category | flops | bytes accessed | tf_op | source)
XLA Modules:
  0.0 93.9 jit_solution(5368784082239987176)
XLA Ops:
  0.0 91.2 %gradient.1 = f32[16,8,16,128]{3,2,1,0:T(8,128)} custom-call(f32[16,8,16,128]{3,2,1,0:T(8,128)} %ctl.1, bf16[16,8,16,128]{3,2,1,0:T(8,128)(2,1)} %bitcast.7, bf16[256,256]{1,0:T(8,128)(2,1)} %latf.1, bf16[512,512]{1,0:T(8,128)(2,1)} %lonf.1, f32[18,32]{1,0:T(8,128)} %bitcast.9, f32[130,256]{1,0:T(8,128)} %bitcast.8, s32[8,1,64]{2,1,0:T(1,128)} %bitcast.10, ...), custom_call_target="tpu_custom_call" | custom-call | tf_op jit(solution)/shard_map/gradient/pallas_call | solution.py:606
  91.2 2.7 %add.3 = f32[16,8,16,128]{3,2,1,0:T(8,128)} add(f32[16,8,16,128]{3,2,1,0:T(8,128)} %ctl.1, f32[16,8,16,128]{3,2,1,0:T(8,128)} %gradient.1) | non-fusion elementwise | flops 262144 | bytes 3145728 | tf_op jit(solution)/shard_map/add | solution.py:628

commit v3 on v2

--- a/solution.py
+++ b/solution.py
@@ -102,11 +102,33 @@
         pltpu.make_async_copy(ref, ref, ssem.at[phase]).wait()
 
     def loop(first, last, body):
-        def step(k, carry):
+        for k in range(first, last):
             body(k)
-            return carry
-
-        lax.fori_loop(first, last, step, 0)
+
+    def around(start, step, size):
+        return lax.rem(start + step, jnp.int32(size))
+
+    def other_lats():
+        if NL % 16:
+            return [(k, None) for k in range(1, NL)]
+        steps = []
+        for u in (4, 3, 5, 2, 6, 1, 7, 0):
+            steps += [(u, 1), (u, 0)]
+        return steps[:-1]
+
+    def lat_at(step):
+        u, flip = step
+        if flip is None:
+            return around(i, u, NL)
+        return around(i // 2, u, NL // 2) * 2 + around(i, flip, 2)
+
+    lat_steps = other_lats()
+    everywhere = [(step, k) for step in lat_steps for k in range(4)]
+    everywhere += [(None, k) for k in (3, 2, 1)]
+
+    def place_at(step_and_k):
+        step, k = step_and_k
+        return (i if step is None else lat_at(step)), around(j, k, 4)
 
     copies = [
         pltpu.make_async_copy(src, dst, lsem.at[n])
@@ -133,24 +155,25 @@
     def hello(*where):
         pl.semaphore_signal(ready, inc=1, device_id=where, device_id_type=MESH)
 
-    loop(1, 4 * NL, lambda k: hello(t, (i + k // 4) % NL, (j + k) % 4))
-    loop(4, 4 * NT, lambda k: hello((t + k // 4) % NT, i, (j + k) % 4))
+    for spot in everywhere:
+        hello(t, *place_at(spot))
+    loop(4, 4 * NT, lambda k: hello(around(t, k // 4, NT), i, around(j, k, 4)))
 
     @pl.when(i < NL - 1)
     def _():
-        loop(2, 2 * NT, lambda k: hello((t + k // 2) % NT, i + 1, (k % 2) * 2))
+        loop(2, 2 * NT, lambda k: hello(around(t, k // 2, NT), i + 1, (k % 2) * 2))
 
         @pl.when(rg == 1)
         def _():
-            loop(2, 2 * NT, lambda k: hello((t + k // 2) % NT, i + 1, (k % 2) * 2 + 1))
+            loop(2, 2 * NT, lambda k: hello(around(t, k // 2, NT), i + 1, (k % 2) * 2 + 1))
 
     @pl.when(i > 0)
     def _():
-        loop(2, 2 * NT, lambda k: hello((t + k // 2) % NT, i - 1, (k % 2) * 2 + 1))
+        loop(2, 2 * NT, lambda k: hello(around(t, k // 2, NT), i - 1, (k % 2) * 2 + 1))
 
         @pl.when(rg == 0)
         def _():
-            loop(2, 2 * NT, lambda k: hello((t + k // 2) % NT, i - 1, (k % 2) * 2))
+            loop(2, 2 * NT, lambda k: hello(around(t, k // 2, NT), i - 1, (k % 2) * 2))
 
     peers = 4 * NL - 1 + 4 * NT - 4
     peers = peers + jnp.where(i < NL - 1, (NT - 1) * (2 + 2 * rg), 0)
@@ -198,23 +221,21 @@
     lat_t = lat_m.astype(F32).T.astype(BF16)
     pl.semaphore_wait(ready, peers)
 
-    def send_a(k):
-        to = (i + k) % NL
+    for step in lat_steps:
+        to = lat_at(step)
         send(cs.at[to], abuf.at[i], 0, (t, to, j))
-
-    loop(1, NL, send_a)
     abuf[i] = cs[i]
 
     def send_o(k):
-        to = (t + k) % NT
+        to = around(t, k, NT)
         send(opk.at[to], obuf.at[t], 1, (to, i, j))
 
     loop(1, NT, send_o)
     obuf[t] = opk[t]
 
     def send_p(k):
-        to = (t + k // 2) % NT
-        half = (rg + k) % 2
+        to = around(t, k // 2, NT)
+        half = around(rg, k, 2)
         send(psend.at[to * 2 + half], pbuf.at[t * 2 + rg], 2, (to, i, ch * 2 + half))
 
     loop(1, 2 * NT, send_p)
@@ -261,12 +282,9 @@
     both = nn(lat_m, jnp.concatenate([high, low], axis=1))
     ybuf[...] = (both[:, :COLS] + both[:, COLS:]).reshape(2 * NL, 8, COLS)
 
-    def send_b(k):
-        lat = (i + k // 4) % NL
-        lon = (j + k) % 4
-        send(ybuf.at[lat * 2 + lon % 2], bbuf.at[j * NL + i], 3, (t, lat, lon))
-
-    loop(1, 4 * NL, send_b)
+    for spot in everywhere:
+        lat, lon = place_at(spot)
+        send(ybuf.at[lat * 2 + around(lon, 0, 2)], bbuf.at[j * NL + i], 3, (t, lat, lon))
     bbuf[j * NL + i] = ybuf[i * 2 + rg]
     arrived(bbuf.at[pl.ds(0, 4 * NL - 1)], 3)
 
@@ -288,30 +306,30 @@
             inc[2 * s + blk] = x
             rows[2 * s + blk] = jnp.where(rg == 0, x[0:1], x[7:8])
 
-    def send_d(k):
-        s = (t + k // 2) % NT
-        lon = ch * 2 + (rg + k) % 2
-        send(inc.at[pl.ds(2 * s, 2)], wown.at[pl.ds((t * 2 + rg) * 2, 2)], 4, (s, i, lon))
-
-    loop(1, 2 * NT, send_d)
+    @pl.when(rim)
+    def _():
+        lat = i + 2 * rg - 1
+        spot = ((1 - rg) * NT + t) * 4 + ch * 2
+
+        def send_f(k):
+            s = around(t, k // 4, NT)
+            send(rows.at[pl.ds(2 * s, 2)], lr.at[pl.ds(spot, 2)], 6 + rg, (s, lat, k % 4))
+
+        loop(0, 4 * NT, send_f)
 
     def send_e(k):
-        s = (t + k // 2) % NT
+        s = around(t, k // 2, NT)
         e = k % 2
         send(inc.at[2 * s + 1 - e], woth.at[t * 2 + rg], 5, (s, i, 2 - 2 * ch + e))
 
     loop(0, 2 * NT, send_e)
 
-    @pl.when(rim)
-    def _():
-        lat = i + 2 * rg - 1
-
-        def send_f(k):
-            s = (t + k // 4) % NT
-            spot = ((1 - rg) * NT + t) * 4 + ch * 2
-            send(rows.at[pl.ds(2 * s, 2)], lr.at[pl.ds(spot, 2)], 6 + rg, (s, lat, k % 4))
-
-        loop(0, 4 * NT, send_f)
+    def send_d(k):
+        s = around(t, k // 2, NT)
+        lon = ch * 2 + around(rg, k, 2)
+        send(inc.at[pl.ds(2 * s, 2)], wown.at[pl.ds((t * 2 + rg) * 2, 2)], 4, (s, i, lon))
+
+    loop(1, 2 * NT, send_d)
 
     wown[(t * 2 + rg) * 2] = inc[2 * t]
     wown[(t * 2 + rg) * 2 + 1] = inc[2 * t + 1]
@@ -365,9 +383,38 @@
         grow[2 * k] = g[inner + k : inner + k + 1, :COLS]
         grow[2 * k + 1] = g[inner + k : inner + k + 1, COLS:]
 
+    def send_rim(pos):
+        def go(k):
+            l = around(t, k // 2, NT)
+            send(
+                grow.at[pl.ds((pos * NT + l) * 2, 2)],
+                glr.at[pl.ds((t * 4 + j) * 2, 2)],
+                10 + pos,
+                (l, i - 1 + 2 * pos, (k % 2) * 2 + 1 - pos),
+            )
+
+        loop(0, 2 * NT, go)
+
+    @pl.when(i > 0)
+    def _():
+        send_rim(0)
+
+    @pl.when(i < NL - 1)
+    def _():
+        send_rim(1)
+
+    def send_h(k):
+        l = around(t, k // 2, NT)
+        half = k % 2
+        send(
+            gb.at[(l * 2 + half) * 2 + 1], goth.at[t * 2 + rg], 9, (l, i, 2 - 2 * ch + half)
+        )
+
+    loop(0, 2 * NT, send_h)
+
     def send_g(k):
-        l = (t + k // 2) % NT
-        half = (rg + k) % 2
+        l = around(t, k // 2, NT)
+        half = around(rg, k, 2)
         send(
             gb.at[pl.ds((l * 2 + half) * 2, 2)],
             gown.at[pl.ds((t * 2 + rg) * 2, 2)],
@@ -376,35 +423,6 @@
         )
 
     loop(1, 2 * NT, send_g)
-
-    def send_h(k):
-        l = (t + k // 2) % NT
-        half = k % 2
-        send(
-            gb.at[(l * 2 + half) * 2 + 1], goth.at[t * 2 + rg], 9, (l, i, 2 - 2 * ch + half)
-        )
-
-    loop(0, 2 * NT, send_h)
-
-    def send_rim(pos):
-        def go(k):
-            l = (t + k // 2) % NT
-            send(
-                grow.at[pl.ds((pos * NT + l) * 2, 2)],
-                glr.at[pl.ds((t * 4 + j) * 2, 2)],
-                10 + pos,
-                (l, i - 1 + 2 * pos, (k % 2) * 2 + 1 - pos),
-            )
-
-        loop(0, 2 * NT, go)
-
-    @pl.when(i > 0)
-    def _():
-        send_rim(0)
-
-    @pl.when(i < NL - 1)
-    def _():
-        send_rim(1)
 
     gown[(t * 2 + rg) * 2] = gb[(t * 2 + rg) * 2]
     gown[(t * 2 + rg) * 2 + 1] = gb[(t * 2 + rg) * 2 + 1]
@@ -447,12 +465,10 @@
     for b in range(4):
         hbuf[NL * b : NL * b + NL] = h[:, b * COLS : (b + 1) * COLS].reshape(NL, 8, COLS)
 
-    def send_c(k):
-        lat = (i + k // 4) % NL
-        lon = (j + k) % 4
+    for spot in everywhere:
+        lat, lon = place_at(spot)
         send(hbuf.at[lon * NL + lat], b2.at[ch * 2 * NL + 2 * i + rg], 12, (t, lat, lon))
 
-    loop(1, 4 * NL, send_c)
     b2[ch * 2 * NL + 2 * i + rg] = hbuf[j * NL + i]
     arrived(b2.at[pl.ds(0, 4 * NL - 1)], 12)
     y = (b2[: 2 * NL] + b2[2 * NL :]).reshape(NL * ROWS, COLS)
@@ -464,11 +480,10 @@
     size = NL // chunks
     own = i // size
 
-    def send_i(k):
-        to = (i + k) % NL
+    for step in lat_steps:
+        to = lat_at(step)
         send(adb.at[to], out.at[i, t], 16 + own, (t, to, j))
 
-    loop(1, NL, send_i)
     out[i, t] = adb[i]
 
     core = t % 2

time: 94 us -> 88.8 us (0.945)
  Pallas kernels: 91.2 us -> 86 us
    pallas_call x1, Pallas kernels: 91.2 us -> 86 us  [per_device(): pl.pallas_call(functools.partial(kernel, NT, NL), name='gradient', out_sh...]
where the time goes in v3:
time: 88.8 us; the launch traced here: 88.7 us
  Pallas kernels  86 us (97%)
  other arithmetic  2.67 us (3%)
    pallas_call x1, Pallas kernels, per_device(): pl.pallas_call(functools.partial(kernel, NT, NL), name='gradient', out_sh...  86 us
    add x1, other arithmetic, per_device(): return control + adjoint  2.67 us

profile of v3, /device:TPU:1, one launch (start us, length us, event | category | flops | bytes accessed | tf_op | source)
XLA Modules:
  0.0 88.7 jit_solution(17450928350640359243)
XLA Ops:
  0.0 86.0 %gradient.1 = f32[16,8,16,128]{3,2,1,0:T(8,128)} custom-call(f32[16,8,16,128]{3,2,1,0:T(8,128)} %ctl.1, bf16[16,8,16,128]{3,2,1,0:T(8,128)(2,1)} %bitcast.7, bf16[256,256]{1,0:T(8,128)(2,1)} %latf.1, bf16[512,512]{1,0:T(8,128)(2,1)} %lonf.1, f32[18,32]{1,0:T(8,128)} %bitcast.9, f32[130,256]{1,0:T(8,128)} %bitcast.8, s32[8,1,64]{2,1,0:T(1,128)} %bitcast.10, ...), custom_call_target="tpu_custom_call" | custom-call | tf_op jit(solution)/shard_map/gradient/pallas_call | solution.py:621
  86.0 2.7 %add.3 = f32[16,8,16,128]{3,2,1,0:T(8,128)} add(f32[16,8,16,128]{3,2,1,0:T(8,128)} %ctl.1, f32[16,8,16,128]{3,2,1,0:T(8,128)} %gradient.1) | non-fusion elementwise | flops 262144 | bytes 3145728 | tf_op jit(solution)/shard_map/add | solution.py:643

commit v4 on v3

--- a/solution.py
+++ b/solution.py
@@ -76,6 +76,7 @@
     hbuf,
     b2,
     adb,
+    gat,
     lsem,
     ssem,
     rsem,
@@ -476,72 +477,75 @@
     both = nn(lat_t, jnp.concatenate([high, low], axis=1))
     adb[...] = (both[:, :COLS] + both[:, COLS:]).reshape(NL, ROWS, COLS)
 
+    for step in lat_steps:
+        to = lat_at(step)
+        send(adb.at[to], gat.at[i, t], 13, (t, to, j))
+
+    gat[i, t] = adb[i]
+
     chunks = 4 if NL % 4 == 0 else NL
     size = NL // chunks
-    own = i // size
-
-    for step in lat_steps:
-        to = lat_at(step)
-        send(adb.at[to], out.at[i, t], 16 + own, (t, to, j))
-
-    out[i, t] = adb[i]
-
-    core = t % 2
+    half = chunks // 2
+    chips = NT // 2
+    core = lax.rem(t, jnp.int32(2))
     sibling = t + 1 - 2 * core
-    right, left = (t + 2) % NT, (t + NT - 2) % NT
-    chips = NT // 2
-    order = (0, 1, 3, 2) if chunks == 4 else tuple(range(chunks))
-    places = [(own + o) % chunks for o in order]
-
-    def chunk(q, owner):
-        return out.at[pl.ds(q * size, size), owner]
-
-    def pass_on(q, owner, n, to):
+    right, left = around(t, 2, NT), around(t, NT - 2, NT)
+    across = around(t, NT // 2, NT)
+
+    def chunk(c, owner):
+        return gat.at[pl.ds(c * size, size), owner]
+
+    def pass_on(ref, n, to):
         pltpu.make_async_remote_copy(
-            src_ref=chunk(q, owner),
-            dst_ref=chunk(q, owner),
+            src_ref=ref,
+            dst_ref=ref,
             send_sem=ssem.at[14],
             recv_sem=hsem.at[n],
             device_id=(to, i, j),
             device_id_type=MESH,
         ).start()
 
-    def landed(q, n):
-        pltpu.make_async_copy(chunk(q, t), chunk(q, t), hsem.at[n]).wait()
+    def landed(c, n):
+        pltpu.make_async_copy(chunk(c, t), chunk(c, t), hsem.at[n]).wait()
+
+    outward = []
+
+    def to_out(owner):
+        n = len(outward)
+        outward.append(pltpu.make_async_copy(gat.at[:, owner], out.at[:, owner], lsem.at[n]))
+        outward[-1].start()
 
     from_left, from_right, from_far, from_sibling = 0, chunks, 2 * chunks, 3 * chunks
-
-    def relay(k):
-        q = places[k]
-        landed(q, from_left + k)
-        if 2 * k < chunks:
-            pass_on(q, left, from_far + k, right)
-        pass_on(q, left, from_sibling, sibling)
-        landed(q, from_right + k)
-        if 2 * k >= chunks:
-            pass_on(q, right, from_far + k, left)
-        pass_on(q, right, from_sibling, sibling)
-
-    for k, q in enumerate(places):
-        if k == 0:
-            if size > 1:
-                arrived(out.at[pl.ds(0, size - 1), t], 16 + q)
-        else:
-            arrived(out.at[pl.ds(0, size), t], 16 + q)
-        if chips > 1:
-            pass_on(q, t, from_left + k, right)
-            pass_on(q, t, from_right + k, left)
-        pass_on(q, t, from_sibling, sibling)
-        if chips > 1 and k > 0:
-            relay(k - 1)
+    rightward = list(range(chunks))
+    leftward = rightward[half:] + rightward[:half]
+    arrived(gat.at[pl.ds(0, NL - 1), t], 13)
     if chips > 1:
-        relay(chunks - 1)
-        across = (t + NT // 2) % NT
-        for k, q in enumerate(places):
-            landed(q, from_far + k)
-            pass_on(q, across, from_sibling, sibling)
-    everything = out.at[:, pl.ds(0, chips)]
+        for c, d in zip(rightward, leftward):
+            pass_on(chunk(c, t), from_left + c, right)
+            pass_on(chunk(d, t), from_right + d, left)
+    pass_on(gat.at[:, t], from_sibling, sibling)
+    to_out(t)
+    if chips > 1:
+        for c, d in zip(rightward, leftward):
+            landed(c, from_left + c)
+            if c < half:
+                pass_on(chunk(c, left), from_far + c, right)
+            pass_on(chunk(c, left), from_sibling, sibling)
+            landed(d, from_right + d)
+            if d >= half:
+                pass_on(chunk(d, right), from_far + d, left)
+            pass_on(chunk(d, right), from_sibling, sibling)
+        to_out(left)
+        to_out(right)
+        for n in range(chunks):
+            c = n // 2 + (n % 2) * half if chunks % 2 == 0 else n
+            landed(c, from_far + c)
+            pass_on(chunk(c, across), from_sibling, sibling)
+        to_out(across)
+    everything = gat.at[:, pl.ds(0, chips)]
     pltpu.make_async_copy(everything, everything, hsem.at[from_sibling]).wait()
+    for chip in range(chips):
+        to_out(2 * chip + 1 - core)
 
     sent(abuf.at[pl.ds(0, NL - 1)], 0)
     sent(obuf.at[pl.ds(0, NT - 1)], 1)
@@ -570,8 +574,10 @@
         sent(lr.at[pl.ds(0, 4 * NT)], 11)
 
     sent(b2.at[pl.ds(0, 4 * NL - 1)], 12)
-    sent(out.at[pl.ds(0, NL - 1), t], 16 + own)
-    sent(out.at[:, pl.ds(0, NT - 1)], 14)
+    sent(gat.at[pl.ds(0, NL - 1), t], 13)
+    sent(gat.at[:, pl.ds(0, NT - 1)], 14)
+    for copy in outward:
+        copy.wait()
 
 
 def per_device(NT, NL, control, pert, latf, lonf, ilat, ilon, cell, count, value, weight):
@@ -613,9 +619,10 @@
         V((4 * NL, *tile), F32),
         V((4 * NL, *tile), F32),
         V((NL, ROWS, COLS), F32),
+        V((NL, NT, ROWS, COLS), F32),
         pltpu.SemaphoreType.DMA((10,)),
-        pltpu.SemaphoreType.DMA((20,)),
-        pltpu.SemaphoreType.DMA((20,)),
+        pltpu.SemaphoreType.DMA((15,)),
+        pltpu.SemaphoreType.DMA((15,)),
         pltpu.SemaphoreType.DMA((13,)),
     ]
     adjoint = pl.pallas_call(
@@ -623,7 +630,7 @@
         name="gradient",
         out_shape=jax.ShapeDtypeStruct(control.shape, F32),
         in_specs=[hbm] * 10,
-        out_specs=pl.BlockSpec(memory_space=pltpu.VMEM),
+        out_specs=hbm,
         scratch_shapes=scratch,
         compiler_params=pltpu.CompilerParams(
             has_side_effects=True, collective_id=0, vmem_limit_bytes=63 * 1024 * 1024

time: 88.8 us -> 86.9 us (0.979)
  Pallas kernels: 86 us -> 84 us
    pallas_call x1, Pallas kernels: 86 us -> 84 us  [per_device(): pl.pallas_call(functools.partial(kernel, NT, NL), name='gradient', out_sh...]
where the time goes in v4:
time: 86.9 us; the launch traced here: 86.7 us
  Pallas kernels  84 us (97%)
  other arithmetic  2.67 us (3%)
    pallas_call x1, Pallas kernels, per_device(): pl.pallas_call(functools.partial(kernel, NT, NL), name='gradient', out_sh...  84 us
    add x1, other arithmetic, per_device(): return control + adjoint  2.67 us

profile of v4, /device:TPU:1, one launch (start us, length us, event | category | flops | bytes accessed | tf_op | source)
XLA Modules:
  0.0 86.7 jit_solution(10572899423251175155)
XLA Ops:
  0.0 84.0 %gradient.1 = f32[16,8,16,128]{3,2,1,0:T(8,128)} custom-call(f32[16,8,16,128]{3,2,1,0:T(8,128)} %ctl.1, bf16[16,8,16,128]{3,2,1,0:T(8,128)(2,1)} %bitcast.7, bf16[256,256]{1,0:T(8,128)(2,1)} %latf.1, bf16[512,512]{1,0:T(8,128)(2,1)} %lonf.1, f32[18,32]{1,0:T(8,128)} %bitcast.9, f32[130,256]{1,0:T(8,128)} %bitcast.8, s32[8,1,64]{2,1,0:T(1,128)} %bitcast.10, ...), custom_call_target="tpu_custom_call" | custom-call | tf_op jit(solution)/shard_map/gradient/pallas_call | solution.py:628
  84.0 2.7 %add.3 = f32[16,8,16,128]{3,2,1,0:T(8,128)} add(f32[16,8,16,128]{3,2,1,0:T(8,128)} %ctl.1, f32[16,8,16,128]{3,2,1,0:T(8,128)} %gradient.1) | non-fusion elementwise | flops 262144 | bytes 3145728 | tf_op jit(solution)/shard_map/add | solution.py:650

commit v5 on v4

--- a/solution.py
+++ b/solution.py
@@ -14,6 +14,7 @@
 ROWS, COLS = 16, 128
 FINE_ROWS, FINE_COLS = 32, 256
 KR = 256
+HELD = 3
 
 
 def halves(x):
@@ -239,7 +240,10 @@
         half = around(rg, k, 2)
         send(psend.at[to * 2 + half], pbuf.at[t * 2 + rg], 2, (to, i, ch * 2 + half))
 
-    loop(1, 2 * NT, send_p)
+    held = [2 * k + 1 for k in dict.fromkeys((0, NT - 1, 1, NT - 2, 2, NT - 3))][:HELD]
+    for k in range(1, 2 * NT):
+        if k not in held:
+            send_p(k)
     pbuf[t * 2 + rg] = psend[t * 2 + rg]
 
     k_row = lax.broadcasted_iota(jnp.int32, (KR, 18), 0)
@@ -275,7 +279,9 @@
     lev = lax.broadcasted_iota(jnp.int32, (KR, n_obs), 0)
     lev = jnp.where(lev < inner, lev >> 4, jnp.where(lev < inner + NT, lev - inner, lev - inner - NT))
     r_mat = nn(p_rows, hot_row, precision=HIGHEST)
-    rtb[...] = jnp.where(lev == o_lev, r_mat, 0.0)
+    high, low = halves(jnp.where(lev == o_lev, r_mat, 0.0))
+    rtb[:KR] = high
+    rtb[KR:] = low
     ctb[...] = nn(q_rows, hot_col, precision=HIGHEST)
 
     arrived(abuf.at[pl.ds(0, NL - 1)], 0)
@@ -286,6 +292,8 @@
     for spot in everywhere:
         lat, lon = place_at(spot)
         send(ybuf.at[lat * 2 + around(lon, 0, 2)], bbuf.at[j * NL + i], 3, (t, lat, lon))
+    for k in held:
+        send_p(k)
     bbuf[j * NL + i] = ybuf[i * 2 + rg]
     arrived(bbuf.at[pl.ds(0, 4 * NL - 1)], 3)
 
@@ -367,7 +375,8 @@
             lane1 == COLS - 1, before, jnp.where(lane1 == 0, after, 0.0)
         )
 
-    r_high, r_low = halves(rtb[...])
+    r_both = rtb[...]
+    r_high, r_low = r_both[:KR], r_both[KR:]
     w_high, w_low = halves(wbuf[...].T)
     both = nn(jnp.concatenate([w_high, w_low], axis=0), r_high)
     mixed = both[:256] + both[256:] + nn(w_high, r_low)
@@ -375,7 +384,7 @@
     seen = jnp.sum(mixed * cols, axis=0, keepdims=True)
     departure = weight * (seen - target)
     d_high, d_low = halves(cols * departure)
-    both = nt(jnp.concatenate([r_high, r_low], axis=0), d_high)
+    both = nt(r_both, d_high)
     g = both[:KR] + both[KR:] + nt(r_high, d_low)
     for k in range(2 * NT):
         gb[2 * k] = g[8 * k : 8 * k + 8, :COLS]
@@ -609,7 +618,7 @@
         V((2 * NT, *tile), F32),
         V((8 * NT, 1, COLS), F32),
         V((KR, 256), F32),
-        V((KR, NT * 64), F32),
+        V((2 * KR, NT * 64), BF16),
         V((256, NT * 64), F32),
         V((4 * NT, *tile), F32),
         V((4 * NT, 1, COLS), F32),

time: 86.9 us -> 84.9 us (0.977)
  Pallas kernels: 84 us -> 82.1 us
    pallas_call x1, Pallas kernels: 84 us -> 82.1 us  [per_device(): pl.pallas_call(functools.partial(kernel, NT, NL), name='gradient', out_sh...]
where the time goes in v5:
time: 84.9 us; the launch traced here: 84.8 us
  Pallas kernels  82.1 us (97%)
  other arithmetic  2.67 us (3%)
    pallas_call x1, Pallas kernels, per_device(): pl.pallas_call(functools.partial(kernel, NT, NL), name='gradient', out_sh...  82.1 us
    add x1, other arithmetic, per_device(): return control + adjoint  2.67 us

profile of v5, /device:TPU:1, one launch (start us, length us, event | category | flops | bytes accessed | tf_op | source)
XLA Modules:
  0.0 84.8 jit_solution(3114637914559721056)
XLA Ops:
  0.0 82.1 %gradient.1 = f32[16,8,16,128]{3,2,1,0:T(8,128)} custom-call(f32[16,8,16,128]{3,2,1,0:T(8,128)} %ctl.1, bf16[16,8,16,128]{3,2,1,0:T(8,128)(2,1)} %bitcast.7, bf16[256,256]{1,0:T(8,128)(2,1)} %latf.1, bf16[512,512]{1,0:T(8,128)(2,1)} %lonf.1, f32[18,32]{1,0:T(8,128)} %bitcast.9, f32[130,256]{1,0:T(8,128)} %bitcast.8, s32[8,1,64]{2,1,0:T(1,128)} %bitcast.10, ...), custom_call_target="tpu_custom_call" | custom-call | tf_op jit(solution)/shard_map/gradient/pallas_call | solution.py:637
  82.1 2.7 %add.3 = f32[16,8,16,128]{3,2,1,0:T(8,128)} add(f32[16,8,16,128]{3,2,1,0:T(8,128)} %ctl.1, f32[16,8,16,128]{3,2,1,0:T(8,128)} %gradient.1) | non-fusion elementwise | flops 262144 | bytes 3145728 | tf_op jit(solution)/shard_map/add | solution.py:659
